TPU v7x, 32 devices: a whole 2x2x4 slice. The times are simulated.
32 devices in a mesh: chan: 4 (over z), tm: 8 (over y, x, core).
Axes of the slice: x: 2, y: 2, z: 4, core: 2. Of those that a mesh axis runs over, the one named last changes fastest.
Arguments:
- voltages: bfloat16 [2, 64, 4, 524288], P(None, 'tm', 'chan'), may hold values from -6 to 6
- antenna_gains: float32 [2, 64, 4], P(None, None, 'chan'), may hold values from -0.75 to 0.75
- chirp_phase: float32 [4, 131072], P('chan'), may hold values from -3.140625 to 3.140625
- offsets: int32 [4], P('chan'), may hold values from 0 to 4095, as said below
- flags: int32 [4, 512], P('chan', 'tm'), may hold values 0 or 1
- sample_phase_bins: int32 [524288], P('tm'), may hold values from 0 to 2047
Outputs:
- dedispersed: bfloat16 [2, 4, 524288], P(None, 'chan', 'tm')
- sk_weight: float32 [4, 512], P('chan', 'tm')
- profile: float32 [4, 2048], P('chan', 'tm')
- band_profile: float32 [2048], P('tm')
Inputs may be any that keep to these rules, and one draw needn't show every extreme that they name: `offsets`: some channel has the offset 4096 - 1.
All inputs are finite; a program needn't handle non-finite values. No bound on the sum of `flags` on one device may be relied on, other than what follows from the above.
Results may differ from a plain program's by a relative error of at most 0.0045.
Values may be sent and summed in bfloat16 or wider, within the bound.
A program may use at most 192 MiB of HBM per device.

v0:
```python
import functools
import math

import jax
import jax.numpy as jnp
import numpy as np
from jax import lax
from jax.experimental import pallas as pl
from jax.experimental.pallas import tpu as pltpu
from jax.sharding import PartitionSpec as P

NFFT = 131072
OFFSET_BOUND = 4096
SKW = 1024
BINS = 2048


SK_WIDTH = 0.05
EPSILON = 1e-06

COLS = 1 << (NFFT.bit_length() - 1) // 2
ROWS = NFFT // COLS
HALF_ROWS = ROWS // 2
HALO_ROWS = OFFSET_BOUND // COLS
WIN_ROWS = SKW // COLS
WINDOWS = HALF_ROWS // WIN_ROWS
LOW_BINS = 32
HIGH_BINS = BINS // LOW_BINS
BEAM_TILE = 8192
ROW_STEP = 8


def shifted(value, axis, steps):
    count = lax.axis_size(axis)
    first, last = (max(0, -steps), min(count, count - steps))
    return lax.ppermute(value, axis, [(source, source + steps) for source in range(first, last)])


def bf16_split(table):
    high = table.astype(jnp.bfloat16)
    low = (table - high.astype(np.float32)).astype(jnp.bfloat16)
    return np.stack([high, low])


def dft_parts(length):
    index = np.arange(length, dtype=np.int64)
    angle = -2.0 * math.pi / length * (index[:, None] * index[None, :] % length)
    real, imag = (np.cos(angle).astype(np.float32), np.sin(angle).astype(np.float32))
    return np.stack([bf16_split(real), bf16_split(imag)])


def twiddle(row_total, col_total):
    turns = np.arange(row_total, dtype=np.int64)[:, None] * np.arange(col_total, dtype=np.int64) % NFFT
    angle = -2.0 * math.pi / NFFT * turns
    return np.stack([np.cos(angle), np.sin(angle)]).astype(np.float32)


def split(value):
    high = value.astype(jnp.bfloat16)
    return high, (value - high.astype(jnp.float32)).astype(jnp.bfloat16)


def three_pass(left, right, dims):
    def product(a, b):
        return lax.dot_general(a, b, (dims, ((), ())), preferred_element_type=jnp.float32)

    return product(left[0], right[0]) + (product(left[0], right[1]) + product(left[1], right[0]))


def table_times(table, pair, dims, sign):
    real, imag = (split(pair[0]), split(pair[1]))
    rr = three_pass(table[0], real, dims)
    ii = three_pass(table[1], imag, dims)
    ri = three_pass(table[0], imag, dims)
    ir = three_pass(table[1], real, dims)
    if sign > 0:
        return rr - ii, ri + ir
    return rr + ii, ri - ir


def cos_sin(angle):
    half = 0.5 * angle
    square = half * half
    sine = jnp.full_like(square, 1.0 / math.factorial(13))
    for power in (11, 9, 7, 5, 3, 1):
        sine = sine * square + (-1.0) ** (power // 2) / math.factorial(power)
    sine = sine * half
    cosine = jnp.full_like(square, 1.0 / math.factorial(12))
    for power in (10, 8, 6, 4, 2, 0):
        cosine = cosine * square + (-1.0) ** (power // 2) / math.factorial(power)
    return 1.0 - 2.0 * sine * sine, 2.0 * sine * cosine


def beam_kernel(weight_ref, volt_ref, out_ref):
    weights = weight_ref[...]
    total = jnp.dot(weights[0], volt_ref[0, 0], preferred_element_type=jnp.float32)
    total += jnp.dot(weights[1], volt_ref[1, 0], preferred_element_type=jnp.float32)
    out_ref[0, 0] = (total[0:2] + (total[2:4] + total[4:6])).astype(jnp.bfloat16)


def beamform(voltages, weights, shards):
    antennas, channels, samples = voltages.shape[1:]
    block = samples // shards
    tile = min(BEAM_TILE, block)
    steps = block // tile
    real, imag = (weights[0], weights[1])
    on_real = jnp.stack([real, imag])
    on_imag = jnp.stack([-imag, real])
    both = jnp.stack([on_real, on_imag])
    first, rest = split(both)
    second = rest
    third = (both - first.astype(jnp.float32) - second.astype(jnp.float32)).astype(jnp.bfloat16)
    table = jnp.concatenate([first, second, third], axis=1)
    table = jnp.moveaxis(table, 3, 0)
    table = jnp.pad(table, ((0, 0), (0, 0), (0, 2), (0, 0)))
    moved = jnp.transpose(voltages, (0, 2, 1, 3))
    outs = []
    for channel in range(channels):
        outs.append(
            pl.pallas_call(
                beam_kernel,
                out_shape=jax.ShapeDtypeStruct((shards, 1, 2, block), jnp.bfloat16),
                grid=(shards * steps,),
                in_specs=[
                    pl.BlockSpec((2, 8, antennas), lambda i: (0, 0, 0)),
                    pl.BlockSpec(
                        (2, 1, antennas, tile), lambda i, channel=channel: (0, channel, 0, i)
                    ),
                ],
                out_specs=pl.BlockSpec((1, 1, 2, tile), lambda i: (i // steps, 0, 0, i % steps)),
                cost_estimate=pl.CostEstimate(
                    flops=64 * samples * antennas,
                    bytes_accessed=4 * samples * antennas,
                    transcendentals=0,
                ),
                name="beam",
            )(table[channel], moved)
        )
    return outs[0] if channels == 1 else jnp.concatenate(outs, axis=1)


def fold_kernel(
    offset_ref, wide_ref, chirp_ref, keep_ref, bins_ref, outer_ref, inner_ref, twist_ref,
    twist_back_ref, dedispersed_ref, weight_ref, profile_ref, weighted_ref,
):
    offset = offset_ref[0]
    whole, part = (offset // COLS, offset % COLS)
    lane = lax.broadcasted_iota(jnp.int32, (ROWS, COLS), 1)
    turn = lax.rem(COLS - part, COLS)
    base = pl.multiple_of(whole // 8 * 8, 8)
    lift = lax.rem(ROWS + 8 - whole % 8, ROWS + 8)
    signal = []
    for half in range(2):
        loaded = wide_ref[half, pl.ds(base, ROWS + 8), :]
        loaded = pltpu.roll(pltpu.roll(loaded, lift, 0), turn, 1)
        signal.append(jnp.where(lane < COLS - part, loaded[:ROWS], loaded[1 : ROWS + 1]))

    def table(ref, rows=slice(None)):
        return [[ref[0, 0, rows], ref[0, 1, rows]], [ref[1, 0, rows], ref[1, 1, rows]]]

    plain, turned = (((1,), (0,)), ((1,), (1,)))
    real, imag = table_times(table(outer_ref), signal, plain, 1)
    cosine, sine = (twist_ref[0], twist_ref[1])
    real, imag = (real * cosine - imag * sine, real * sine + imag * cosine)
    real, imag = table_times(table(inner_ref), (real, imag), turned, 1)
    cosine, sine = cos_sin(chirp_ref[...])
    real, imag = (real * cosine - imag * sine, real * sine + imag * cosine)
    real, imag = table_times(table(inner_ref), (real, imag), plain, -1)
    cosine, sine = (twist_back_ref[0], twist_back_ref[1])
    real, imag = (real * cosine + imag * sine, imag * cosine - real * sine)
    real, imag = table_times(
        table(outer_ref, slice(HALF_ROWS, ROWS)), (real, imag), turned, -1
    )
    real, imag = (real * (1.0 / NFFT), imag * (1.0 / NFFT))
    dedispersed_ref[0] = real.astype(jnp.bfloat16)
    dedispersed_ref[1] = imag.astype(jnp.bfloat16)
    power = real * real + imag * imag

    def exact_dot(a, b):
        return jnp.dot(a, b, precision=lax.Precision.HIGHEST, preferred_element_type=jnp.float32)

    def owner(shape, axis):
        rows = lax.broadcasted_iota(jnp.int32, shape, axis)
        windows = lax.broadcasted_iota(jnp.int32, shape, 1 - axis)
        return jnp.where(rows // WIN_ROWS == windows, 1.0, 0.0).astype(jnp.float32)

    gather = owner((WINDOWS, HALF_ROWS), 1)
    first_sum = jnp.sum(exact_dot(gather, power), axis=1, keepdims=True)
    second_sum = jnp.sum(exact_dot(gather, power * power), axis=1, keepdims=True)
    kurtosis = (
        (SKW + 1.0) / (SKW - 1.0) * (SKW * second_sum / (first_sum * first_sum + EPSILON) - 1.0)
    )
    scaled = (kurtosis - 1.0) / SK_WIDTH
    sk_weight = keep_ref[...] / (1.0 + scaled * scaled)
    sk_weight = jnp.broadcast_to(sk_weight, (WINDOWS, COLS))
    weight_ref[...] = sk_weight[:, :128]
    spread_weight = exact_dot(owner((HALF_ROWS, WINDOWS), 0), sk_weight)
    weighted_ref[...] = (spread_weight * power).astype(jnp.bfloat16).astype(jnp.float32)

    high_index = lax.broadcasted_iota(jnp.int32, (HIGH_BINS, COLS), 0)
    low_index = lax.broadcasted_iota(jnp.int32, (LOW_BINS, COLS), 0)

    def step(at, total):
        rows = pl.ds(pl.multiple_of(at * ROW_STEP, ROW_STEP), ROW_STEP)
        bins, values = (bins_ref[rows, :], weighted_ref[rows, :])
        high, low = (bins // LOW_BINS, bins % LOW_BINS)
        left, right = ([], [])
        for row in range(ROW_STEP):
            left.append(
                jnp.where(high_index == high[row : row + 1], 1.0, 0.0).astype(jnp.bfloat16)
            )
            right.append(
                jnp.where(low_index == low[row : row + 1], values[row : row + 1], 0.0).astype(
                    jnp.bfloat16
                )
            )
        return total + lax.dot_general(
            jnp.concatenate(left, axis=1),
            jnp.concatenate(right, axis=1),
            (turned, ((), ())),
            preferred_element_type=jnp.float32,
        )

    profile_ref[...] = lax.fori_loop(
        0, HALF_ROWS // ROW_STEP, step, jnp.zeros((HIGH_BINS, LOW_BINS), jnp.float32)
    )


def fold(offset, wide, chirp, keep, bins):
    vmem = pl.BlockSpec(memory_space=pltpu.VMEM)
    tables = (dft_parts(ROWS), dft_parts(COLS), twiddle(ROWS, COLS), twiddle(COLS, ROWS))
    return pl.pallas_call(
        fold_kernel,
        out_shape=(
            jax.ShapeDtypeStruct((2, HALF_ROWS, COLS), jnp.bfloat16),
            jax.ShapeDtypeStruct((WINDOWS, 128), jnp.float32),
            jax.ShapeDtypeStruct((HIGH_BINS, LOW_BINS), jnp.float32),
        ),
        in_specs=[pl.BlockSpec(memory_space=pltpu.SMEM)] + [vmem] * 8,
        out_specs=(vmem,) * 3,
        scratch_shapes=[pltpu.VMEM((HALF_ROWS, COLS), jnp.float32)],
        compiler_params=pltpu.CompilerParams(vmem_limit_bytes=40 << 20),
        cost_estimate=pl.CostEstimate(
            flops=6 * 10**9, bytes_accessed=6 << 20, transcendentals=0
        ),
        name="fold",
    )(offset, wide, chirp, keep, bins, *[jnp.asarray(table) for table in tables])


def on_device(voltages, antenna_gains, chirp_phase, offsets, flags, sample_phase_bins):
    shards = lax.axis_size("tm")
    my_index = lax.axis_index("tm")
    half_length = NFFT // 2
    channels_here = voltages.shape[2]
    antennas_here = voltages.shape[1]
    own_weights = lax.dynamic_slice_in_dim(
        antenna_gains, my_index * antennas_here, antennas_here, 1
    )
    partial_beam = beamform(voltages, own_weights, shards)
    pieces = lax.all_to_all(partial_beam, "tm", 0, 0, tiled=True)
    beam_sum = jnp.sum(pieces.astype(jnp.float32), axis=0)
    beam_sum = beam_sum.reshape(channels_here, 2, HALF_ROWS, COLS)
    earlier = shifted(beam_sum, "tm", 1)
    later = shifted(beam_sum[:, :, :HALO_ROWS], "tm", -1)
    wide = jnp.concatenate([earlier, beam_sum, later], axis=2)
    chirp = chirp_phase.reshape(channels_here, COLS, ROWS)
    keep = (1 - flags).astype(jnp.float32)[:, :, None]
    bins = sample_phase_bins.reshape(HALF_ROWS, COLS)
    results = [
        fold(offsets[at : at + 1], wide[at], chirp[at], keep[at], bins)
        for at in range(channels_here)
    ]
    dedispersed = jnp.stack([item[0].reshape(2, half_length) for item in results], axis=1)
    sk_weight = jnp.stack([item[1][:, 0] for item in results])
    partial_profile = jnp.stack([item[2].reshape(BINS) for item in results])
    blocks = jnp.moveaxis(partial_profile.reshape(channels_here, shards, BINS // shards), 1, 0)
    gathered = lax.all_to_all(blocks, "tm", 0, 0, tiled=True)
    profile = jnp.sum(gathered, axis=0) * (BINS / (half_length * shards))
    band_profile = jnp.sum(lax.all_gather(jnp.sum(profile, axis=0), "chan"), axis=0)
    return (dedispersed, sk_weight, profile, band_profile)


def solution(mesh):
    placed = (
        P(None, "tm", "chan", None),
        P(None, None, "chan"),
        P("chan", None),
        P("chan"),
        P("chan", "tm"),
        P("tm"),
    )
    return jax.shard_map(
        on_device,
        mesh=mesh,
        in_specs=placed,
        out_specs=(P(None, "chan", "tm"), P("chan", "tm"), P("chan", "tm"), P("tm")),
        check_vma=False,
    )
```

profile of v0, /device:TPU:0, one launch (start us, length us, event | category | flops | bytes accessed | tf_op | source)
XLA Modules:
  0.0 128.3 jit_solution(14858967377195843959)
XLA Ops:
  0.6 0.8 constant_dynamic-slice_fusion.2
  1.4 0.7 fusion.1
  2.2 0.6 pad_bitcast_fusion.weight_ref
  2.8 41.8 %beam.1 = bf16[8,1,2,65536]{3,2,1,0:T(2,128)(2,1)} custom-call(bf16[2,8,8]{2,1,0:T(8,128)(2,1)} %pad_bitcast_fusion.weight_ref, bf16[2,1,8,524288]{3,2,1,0:T(8,128)(2,1)} %bitcast.20), custom_call_target="tpu_custom_call" | custom-call | flops 268435456 | bytes 16777216 | tf_op jit(solution)/shard_map/beam/pallas_call | solution.py:120
  44.6 31.8 %all_to_all.10 = bf16[8,1,2,65536]{3,2,1,0:T(2,128)(2,1)S(1)} all-to-all(bf16[8,1,2,65536]{3,2,1,0:T(2,128)(2,1)} %beam.1), channel_id=1, replica_groups=mesh['chan'=4,'tm'=8] {'tm'}, dimensions={0} | all-to-all | bytes 4194304 | tf_op jit(solution)/shard_map/all_to_all | solution.py:260
  76.3 1.9 %convert_reduce_fusion = f32[2,65536]{1,0:T(2,128)S(1)} fusion(bf16[8,1,2,65536]{3,2,1,0:T(2,128)(2,1)S(1)} %all_to_all.10), kind=kLoop, calls=%fused_computation | loop fusion | flops 1966080 | bytes 2621440 | tf_op jit(solution)/shard_map/reduce_sum | solution.py:261
  78.2 0.8 copy.28
  79.1 2.1 %collective-permute-start = (f32[1,2,256,256]{3,2,1,0:T(8,128)}, f32[1,2,256,256]{3,2,1,0:T(8,128)}, u32[]{:S(2)}, u32[]{:S(2)}) collective-permute-start(f32[1,2,256,256]{3,2,1,0:T(8,128)} %bitcast.18), channel_id=1, source_target_pairs={{0,1},{1,2},{2,3},{3,4},{4,5},{5,6},{6,7},{8,9},{9,10},{10,11},{11... | collective-permute-start | bytes 1572872 | tf_op jit(solution)/shard_map/ppermute | solution.py:36
  81.1 0.8 slice.17
  81.9 1.3 collective-permute-start.1
  83.2 0.5 broadcast.17
  83.7 1.9 %reduce.8 = f32[131072]{0:T(1024)S(1)} reduce(f32[1,131072]{1,0:T(1,128)S(1)} %copy-done.4, f32[]{:T(128)} %broadcast.17), dimensions={0}, to_apply=%param.12.reduce_sub_computation.3 | reduce | bytes 1048580 | tf_op args[2]
  85.7 1.2 reshape.174.bins_ref
  87.8 1.3 maximum_bitcast_fusion.wide_ref
  89.1 1.2 copy-done.2
  90.3 1.0 copy-done.3
  91.3 14.6 %fold.1 = (bf16[2,256,256]{2,1,0:T(8,128)(2,1)S(1)}, f32[64,128]{1,0:T(8,128)S(1)}, f32[64,32]{1,0:T(8,128)S(1)}) custom-call(s32[1]{0:T(128)S(6)} %copy.30.offset_ref, f32[2,528,256]{2,1,0:T(8,128)S(1)} %maximum_bitcast_fusion.wide_ref, f32[256,512]{1,0:T(8,128)S(1)} %squeeze_reshape.3.chirp_ref, f32[64,1]{1,0:T(8,128)S(1)} %copy.22.keep_ref, ...), custom_call_target="tpu_custom_call" | custom-call | flops 6000000000 | bytes 6291456 | tf_op jit(solution)/shard_map/fold/pallas_call | solution.py:232
  106.0 0.7 transpose_reshape_stack_reshape.4
  106.6 5.2 %all-to-all-start.1 = ((f32[8,1,256]{2,1,0:T(1,128)}), f32[8,1,256]{2,1,0:T(1,128)S(1)}, u32[]{:S(2)}, u32[]{:S(2)}) async-start(f32[8,1,256]{2,1,0:T(1,128)} %transpose_reshape_stack_reshape.4), calls=%async_computation.1 | async-start | bytes 16384 | tf_op jit(solution)/shard_map/all_to_all | solution.py:277
  111.8 0.6 slice_reduce_fusion
  112.4 0.8 stack_reshape.3
  113.2 3.3 %all-to-all-done.1 = f32[8,1,256]{2,1,0:T(1,128)S(1)} async-done(((f32[8,1,256]{2,1,0:T(1,128)}), f32[8,1,256]{2,1,0:T(1,128)S(1)}, u32[]{:S(2)}, u32[]{:S(2)}) %all-to-all-start.1) | async-done | bytes 8224 | tf_op jit(solution)/shard_map/all_to_all | solution.py:277
  116.6 11.2 %all-gather.1 = f32[4,1,256]{2,1,0:T(1,128)S(1)} all-gather(f32[1,1,256]{2,1,0:T(1,128)S(1)} %bitcast.27), channel_id=2, replica_groups=mesh['chan'=4,'tm'=8] {'chan'}, dimensions={0}, use_global_device_ids=true | all-gather | bytes 5120 | tf_op jit(solution)/shard_map/all_gather | solution.py:279
  127.8 0.6 reduce_sum.33
  (25 shorter events, 0.3 us)
Async XLA Ops:
  76.3 6.9 %copy-start.6 = (s32[1,64]{1,0:T(1,128)S(1)}, s32[1,64]{1,0:T(1,128)}, u32[]{:S(2)}) copy-start(s32[1,64]{1,0:T(1,128)} %param.14) | copy-start | bytes 772
  76.3 7.4 %copy-start.4 = (f32[1,131072]{1,0:T(1,128)S(1)}, f32[1,131072]{1,0:T(1,128)}, u32[]{:S(2)}) copy-start(f32[1,131072]{1,0:T(1,128)} %param.12) | copy-start | bytes 1572868
  79.1 8.7 %collective-permute-start = (f32[1,2,256,256]{3,2,1,0:T(8,128)}, f32[1,2,256,256]{3,2,1,0:T(8,128)}, u32[]{:S(2)}, u32[]{:S(2)}) collective-permute-start(f32[1,2,256,256]{3,2,1,0:T(8,128)} %bitcast.18), channel_id=1, source_target_pairs={{0,1},{1,2},{2,3},{3,4},{4,5},{5,6},{6,7},{8,9},{9,10},{10,11},{11... | collective-permute-start | bytes 1572872 | tf_op jit(solution)/shard_map/ppermute | solution.py:36
  81.9 5.8 %collective-permute-start.1 = (f32[1,2,16,256]{3,2,1,0:T(8,128)S(1)}, f32[1,2,16,256]{3,2,1,0:T(8,128)S(1)}, u32[]{:S(2)}, u32[]{:S(2)}) collective-permute-start(f32[1,2,16,256]{3,2,1,0:T(8,128)S(1)} %slice.17), channel_id=1, source_target_pairs={{1,0},{2,1},{3,2},{4,3},{5,4},{6,5},{7,6},{9,8},{10,9},{11,10},{12... | collective-permute-start | bytes 98312 | tf_op jit(solution)/shard_map/ppermute | solution.py:36
  85.6 3.4 %copy-start = (bf16[2,2,512,512]{3,2,1,0:T(8,128)(2,1)S(1)}, bf16[2,2,512,512]{3,2,1,0:T(8,128)(2,1)}, u32[]{:S(2)}) copy-start(bf16[2,2,512,512]{3,2,1,0:T(8,128)(2,1)} %constant.26.clone.outer_ref) | copy-start | bytes 6291460
  87.0 2.1 %copy-start.1 = (f32[2,512,256]{2,1,0:T(8,128)S(1)}, f32[2,512,256]{2,1,0:T(8,128)}, u32[]{:S(2)}) copy-start(f32[2,512,256]{2,1,0:T(8,128)} %constant.28.clone.twist_ref) | copy-start | bytes 3145732
  89.1 1.2 copy-start.2
  90.3 1.0 copy-start.3
  106.6 9.9 %all-to-all-start.1 = ((f32[8,1,256]{2,1,0:T(1,128)}), f32[8,1,256]{2,1,0:T(1,128)S(1)}, u32[]{:S(2)}, u32[]{:S(2)}) async-start(f32[8,1,256]{2,1,0:T(1,128)} %transpose_reshape_stack_reshape.4), calls=%async_computation.1 | async-start | bytes 16384 | tf_op jit(solution)/shard_map/all_to_all | solution.py:277
  116.6 11.8 %copy-start.5 = (f32[256]{0:T(256)}, f32[256]{0:T(256)S(1)}, u32[]{:S(2)}) copy-start(f32[256]{0:T(256)S(1)} %broadcast_multiply_fusion) | copy-start | bytes 3076
where the time goes:
time: 130 us; the launch traced here: 128 us
  Pallas kernels  56.4 us (43%)
  blocking collectives  42.9 us (33%)
  local copies, waits for them, and re-layouts  9.16 us (7%)
  starting transfers between devices  8.55 us (7%)
  other arithmetic  6.44 us (5%)
  waiting for transfers between devices  3.32 us (3%)
  between operations  1.53 us (1%)
    pallas_call x1, Pallas kernels, beamform(): pl.pallas_call(beam_kernel, out_shape=jax.ShapeDtypeStruct((shards, 1, 2,...  41.8 us
    all_to_all x1, blocking collectives, on_device(): pieces = lax.all_to_all(partial_beam, 'tm', 0, 0, tiled=True)  31.8 us
    pallas_call x1, Pallas kernels, fold(): pl.pallas_call(fold_kernel, out_shape=(jax.ShapeDtypeStruct((2, HALF_ROWS...  14.6 us
    all_gather x1, blocking collectives, on_device(): lax.all_gather(jnp.sum(profile, axis=0), 'chan')  11.2 us
    all_to_all x1, starting transfers between devices, on_device(): gathered = lax.all_to_all(blocks, 'tm', 0, 0, tiled=True)  5.17 us
    unnamed x17, local copies, waits for them, and re-layouts  3.63 us
    ppermute x2, starting transfers between devices, shifted(): lax.ppermute(value, axis, [(source, source + steps) for source in range(f...  3.38 us
    all_to_all x1, waiting for transfers between devices, on_device(): gathered = lax.all_to_all(blocks, 'tm', 0, 0, tiled=True)  3.31 us
  transfers between devices with their start and end apart: 3, of which 1 were waited for; matrix products, arithmetic and copies ran while one was open for 5% of the time, Pallas kernels for 0%

commit v1 on v0

v1 whole, which is shorter than its diff:
```python
import functools
import math

import jax
import jax.numpy as jnp
import numpy as np
from jax import lax
from jax.experimental import pallas as pl
from jax.experimental.pallas import tpu as pltpu
from jax.sharding import PartitionSpec as P

NFFT = 131072
OFFSET_BOUND = 4096
SKW = 1024
BINS = 2048


SK_WIDTH = 0.05
EPSILON = 1e-06

COLS = 1 << (NFFT.bit_length() - 1) // 2
ROWS = NFFT // COLS
HALF_ROWS = ROWS // 2
HALO_ROWS = OFFSET_BOUND // COLS
WIN_ROWS = SKW // COLS
WINDOWS = HALF_ROWS // WIN_ROWS
LOW_BINS = 32
HIGH_BINS = BINS // LOW_BINS
ROW_STEP = 8
LANES = 128
DEPTH = 256
PARTS = 4
PART_ROWS = HALF_ROWS // PARTS
MESH = pl.DeviceIdType.MESH


def bf16_split(table):
    high = table.astype(jnp.bfloat16)
    low = (table - high.astype(np.float32)).astype(jnp.bfloat16)
    return np.stack([high, low])


def dft_parts(length):
    index = np.arange(length, dtype=np.int64)
    angle = -2.0 * math.pi / length * (index[:, None] * index[None, :] % length)
    real, imag = (np.cos(angle).astype(np.float32), np.sin(angle).astype(np.float32))
    return np.stack([bf16_split(real), bf16_split(imag)])


def twiddle(row_total, col_total):
    turns = np.arange(row_total, dtype=np.int64)[:, None] * np.arange(col_total, dtype=np.int64) % NFFT
    angle = -2.0 * math.pi / NFFT * turns
    return np.stack([np.cos(angle), np.sin(angle)]).astype(np.float32)


def split(value):
    high = value.astype(jnp.bfloat16)
    return high, (value - high.astype(jnp.float32)).astype(jnp.bfloat16)


def three_pass(left, right, dims):
    def product(a, b):
        return lax.dot_general(a, b, (dims, ((), ())), preferred_element_type=jnp.float32)

    return product(left[0], right[0]) + (product(left[0], right[1]) + product(left[1], right[0]))


def table_times(table, pair, dims, sign):
    real, imag = (split(pair[0]), split(pair[1]))
    rr = three_pass(table[0], real, dims)
    ii = three_pass(table[1], imag, dims)
    ri = three_pass(table[0], imag, dims)
    ir = three_pass(table[1], real, dims)
    if sign > 0:
        return rr - ii, ri + ir
    return rr + ii, ri - ir


def cos_sin(angle):
    half = 0.5 * angle
    square = half * half
    sine = jnp.full_like(square, 1.0 / math.factorial(13))
    for power in (11, 9, 7, 5, 3, 1):
        sine = sine * square + (-1.0) ** (power // 2) / math.factorial(power)
    sine = sine * half
    cosine = jnp.full_like(square, 1.0 / math.factorial(12))
    for power in (10, 8, 6, 4, 2, 0):
        cosine = cosine * square + (-1.0) ** (power // 2) / math.factorial(power)
    return 1.0 - 2.0 * sine * sine, 2.0 * sine * cosine


def shifted_phase(phase, offset):
    high = lax.broadcasted_iota(jnp.int32, phase.shape, 0) * ROWS
    index = high + lax.broadcasted_iota(jnp.int32, phase.shape, 1)
    turns = (index * offset) & (NFFT - 1)
    turns = jnp.where(turns >= NFFT // 2, turns - NFFT, turns)
    phase = phase + turns.astype(jnp.float32) * (2.0 * math.pi / NFFT)
    phase = jnp.where(phase > math.pi, phase - 2.0 * math.pi, phase)
    return jnp.where(phase < -math.pi, phase + 2.0 * math.pi, phase)


def weight_table(gains_ref, table_ref, antennas, me):
    total = gains_ref.shape[2]
    lane = lax.broadcasted_iota(jnp.int32, (8, LANES), 1)
    wide = []
    for part in range(2):
        row = gains_ref[part]
        if total < LANES:
            row = jnp.concatenate([row, jnp.zeros((1, LANES - total), jnp.float32)], axis=1)
        row = jnp.broadcast_to(row, (8, LANES))
        row = pltpu.roll(row, lax.rem(LANES - me * antennas, LANES), 1)
        row = jnp.where(lane < antennas, row, 0.0)
        width = antennas
        while width < LANES:
            row = row + pltpu.roll(row, width, 1)
            width *= 2
        wide.append(jnp.concatenate([row] * (DEPTH // LANES), axis=1)[:1])
    real, imag = wide
    half = DEPTH // antennas // 2
    shape = (half, DEPTH)
    tile = lax.broadcasted_iota(jnp.int32, shape, 1) // antennas
    index = lax.broadcasted_iota(jnp.int32, shape, 0)
    for source, pair in enumerate(((real, imag), (-imag, real))):
        for out, values in enumerate(pair):
            for parity in range(2):
                dense = jnp.where(tile == 2 * index + parity, values, 0.0)
                high, low = split(dense)
                at = (2 * out + parity) * half
                table_ref[source, at : at + half] = high
                table_ref[source, 4 * half + at : 4 * half + at + half] = low


def part_beam(table_ref, volt_ref, antennas, put):
    half = DEPTH // antennas // 2
    groups = volt_ref.shape[1] // DEPTH
    joined = 2 if groups % 2 == 0 else 1
    for at in range(groups // joined):
        total = None
        for source in range(2):
            lanes = [
                volt_ref[source, (joined * at + b) * DEPTH : (joined * at + b + 1) * DEPTH]
                for b in range(joined)
            ]
            right = lanes[0] if joined == 1 else jnp.concatenate(lanes, axis=1)
            term = jnp.dot(table_ref[source], right, preferred_element_type=jnp.float32)
            total = term if total is None else total + term
        total = total[: 4 * half] + total[4 * half :]
        for b in range(joined):
            block = total[:, b * LANES : (b + 1) * LANES]
            for out in range(2):
                even = block[2 * out * half : (2 * out + 1) * half]
                odd = block[(2 * out + 1) * half : (2 * out + 2) * half]
                put(out, (joined * at + b) * half, half, jnp.concatenate([even, odd], axis=1))


def beam_kernel(
    antennas, pairs, volt_ref, gains_ref, wide_ref, table_ref, vbuf, pair_send, pair_recv,
    chip_send, chip_recv, own_ref, halo_ref, head_ref, load_sem, pair_sems, chip_sems, halo_sems,
    head_sems,
):
    count = 2 * pairs
    me = lax.axis_index("tm")
    pair, core = (me // 2, lax.rem(me, 2))
    barrier = pltpu.get_barrier_semaphore()
    for step in range(1, count):
        pl.semaphore_signal(
            barrier, inc=1, device_id={"tm": lax.rem(me + step, count)}, device_id_type=MESH
        )
    size = vbuf.shape[3]

    def shard_of(j, other):
        return lax.rem(pair + 1 + j, pairs) * 2 + (1 - core if other else core)

    def load(part, j, other):
        start = pl.multiple_of((shard_of(j, other) * PARTS + part) * size, size)
        slot = 2 * j + (0 if other else 1)
        return pltpu.make_async_copy(
            volt_ref.at[:, pl.ds(start, size)], vbuf.at[part, slot], load_sem.at[part, slot]
        )

    def order():
        return [(j, True) for j in range(pairs)] + [(j, False) for j in range(pairs)]

    def begin(part, carry):
        for j, other in order():
            load(part, j, other).start()
        return carry

    lax.fori_loop(0, PARTS, begin, 0)
    weight_table(gains_ref, table_ref, antennas, me)

    def pair_copy(part, j):
        return pltpu.make_async_remote_copy(
            src_ref=pair_send.at[part, j], dst_ref=pair_recv.at[part, j],
            send_sem=pair_sems.at[0, part, j], recv_sem=pair_sems.at[1, part, j],
            device_id={"tm": pair * 2 + (1 - core)}, device_id_type=MESH,
        )

    def chip_copy(part, j):
        return pltpu.make_async_remote_copy(
            src_ref=chip_send.at[part, j], dst_ref=chip_recv.at[part, j],
            send_sem=chip_sems.at[0, part, j], recv_sem=chip_sems.at[1, part, j],
            device_id={"tm": shard_of(j, False)}, device_id_type=MESH,
        )

    def halo_copy(part):
        return pltpu.make_async_remote_copy(
            src_ref=own_ref.at[part], dst_ref=halo_ref.at[part],
            send_sem=halo_sems.at[0, part], recv_sem=halo_sems.at[1, part],
            device_id={"tm": lax.rem(me + 1, count)}, device_id_type=MESH,
        )

    def head_copy():
        return pltpu.make_async_remote_copy(
            src_ref=own_ref.at[0, :, 0:HALO_ROWS], dst_ref=head_ref,
            send_sem=head_sems.at[0], recv_sem=head_sems.at[1],
            device_id={"tm": lax.rem(me + count - 1, count)}, device_id_type=MESH,
        )

    def finish(part):
        for j in range(pairs - 1):
            chip_copy(part, j).wait_recv()
        total = own_ref[part]
        for j in range(pairs - 1):
            total = total + chip_recv[part, j].astype(jnp.float32)
        own_ref[part] = total
        rows = pl.ds(pl.multiple_of(HALF_ROWS + part * PART_ROWS, PART_ROWS), PART_ROWS)
        wide_ref[:, rows] = total

        @pl.when(me < count - 1)
        def _():
            halo_copy(part).start()

    def run(part, carry):
        for j in range(pairs):
            load(part, j, True).wait()

            def put(out, at, rows, value, j=j):
                pair_send[part, j, out, at : at + rows] = value

            part_beam(table_ref, vbuf.at[part, 2 * j], antennas, put)
            if j == 0:

                @pl.when(part == 0)
                def _():
                    pl.semaphore_wait(barrier, count - 1)

            pair_copy(part, j).start()
        for j in range(pairs):
            load(part, j, False).wait()
            pair_copy(part, j).wait_recv()
            if j < pairs - 1:

                def put(out, at, rows, value, j=j):
                    value = value + pair_recv[part, j, out, at : at + rows]
                    chip_send[part, j, out, at : at + rows] = value.astype(jnp.bfloat16)

            else:

                def put(out, at, rows, value, j=j):
                    value = value + pair_recv[part, j, out, at : at + rows]
                    own_ref[part, out, at : at + rows] = value

            part_beam(table_ref, vbuf.at[part, 2 * j + 1], antennas, put)
            if j < pairs - 1:
                chip_copy(part, j).start()

        @pl.when(part > 0)
        def _():
            finish(part - 1)

            @pl.when((part == 1) & (me > 0))
            def _():
                head_copy().start()

        return carry

    lax.fori_loop(0, PARTS, run, 0)
    finish(PARTS - 1)

    @pl.when(me > 0)
    def _():
        for part in range(PARTS):
            halo_copy(part).wait_recv()
            wide_ref[:, part * PART_ROWS : (part + 1) * PART_ROWS] = halo_ref[part]
        head_copy().wait_send()

    @pl.when(me == 0)
    def _():
        wide_ref[:, 0:HALF_ROWS] = jnp.zeros((2, HALF_ROWS, COLS), jnp.float32)

    @pl.when(me < count - 1)
    def _():
        head_copy().wait_recv()
        wide_ref[:, ROWS : ROWS + HALO_ROWS] = head_ref[...]
        for part in range(PARTS):
            halo_copy(part).wait_send()

    @pl.when(me == count - 1)
    def _():
        wide_ref[:, ROWS : ROWS + HALO_ROWS] = jnp.zeros((2, HALO_ROWS, COLS), jnp.float32)

    def drain(part, carry):
        for j in range(pairs):
            pair_copy(part, j).wait_send()
            if j < pairs - 1:
                chip_copy(part, j).wait_send()
        return carry

    lax.fori_loop(0, PARTS, drain, 0)


def beam(volts, gains, antennas, shards):
    pairs = shards // 2
    size = volts.shape[1] // shards // PARTS
    half = DEPTH // antennas // 2
    block = (2, PART_ROWS, COLS)
    vmem = pl.BlockSpec(memory_space=pltpu.VMEM)
    return pl.pallas_call(
        functools.partial(beam_kernel, antennas, pairs),
        out_shape=jax.ShapeDtypeStruct((2, ROWS + HALO_ROWS, COLS), jnp.float32),
        in_specs=[pl.BlockSpec(memory_space=pl.ANY), vmem],
        out_specs=vmem,
        scratch_shapes=[
            pltpu.VMEM((2, 8 * half, DEPTH), jnp.bfloat16),
            pltpu.VMEM((PARTS, shards, 2, size, LANES), jnp.bfloat16),
            pltpu.VMEM((PARTS, pairs) + block, jnp.float32),
            pltpu.VMEM((PARTS, pairs) + block, jnp.float32),
            pltpu.VMEM((PARTS, pairs - 1) + block, jnp.bfloat16),
            pltpu.VMEM((PARTS, pairs - 1) + block, jnp.bfloat16),
            pltpu.VMEM((PARTS,) + block, jnp.float32),
            pltpu.VMEM((PARTS,) + block, jnp.float32),
            pltpu.VMEM((2, HALO_ROWS, COLS), jnp.float32),
            pltpu.SemaphoreType.DMA((PARTS, shards)),
            pltpu.SemaphoreType.DMA((2, PARTS, pairs)),
            pltpu.SemaphoreType.DMA((2, PARTS, pairs - 1)),
            pltpu.SemaphoreType.DMA((2, PARTS)),
            pltpu.SemaphoreType.DMA((2,)),
        ],
        compiler_params=pltpu.CompilerParams(
            vmem_limit_bytes=40 << 20, collective_id=0, has_side_effects=True
        ),
        cost_estimate=pl.CostEstimate(
            flops=3 * 10**9, bytes_accessed=18 << 20, transcendentals=0
        ),
        name="beam",
    )(volts, gains)


def fold_kernel(
    chans, shards, offset_ref, wide_ref, chirp_ref, keep_ref, bins_ref, outer_ref, inner_ref,
    twist_ref, twist_back_ref, dedispersed_ref, weight_ref, profile_ref, band_ref, weighted_ref,
    send_ref, recv_ref, sems,
):
    everyone = chans * shards
    here = lax.axis_index("chan") * shards + lax.axis_index("tm")
    barrier = pltpu.get_barrier_semaphore()

    def target(index):
        return {"chan": index // shards, "tm": lax.rem(index, shards)}

    def greet(step, carry):
        pl.semaphore_signal(
            barrier, inc=1, device_id=target(lax.rem(here + step, everyone)), device_id_type=MESH
        )
        return carry

    lax.fori_loop(1, everyone, greet, 0)
    offset = offset_ref[0]
    spot = lax.broadcasted_iota(jnp.int32, (HALO_ROWS, COLS), 0) * COLS
    spot = spot + lax.broadcasted_iota(jnp.int32, (HALO_ROWS, COLS), 1)
    signal = []
    for half in range(2):
        first = jnp.where(spot < offset, wide_ref[half, ROWS:], wide_ref[half, :HALO_ROWS])
        signal.append(jnp.concatenate([first, wide_ref[half, HALO_ROWS:ROWS]], axis=0))

    def table(ref, rows=slice(None)):
        return [[ref[0, 0, rows], ref[0, 1, rows]], [ref[1, 0, rows], ref[1, 1, rows]]]

    plain, turned = (((1,), (0,)), ((1,), (1,)))
    real, imag = table_times(table(outer_ref), signal, plain, 1)
    cosine, sine = (twist_ref[0], twist_ref[1])
    real, imag = (real * cosine - imag * sine, real * sine + imag * cosine)
    real, imag = table_times(table(inner_ref), (real, imag), turned, 1)
    cosine, sine = cos_sin(shifted_phase(chirp_ref[...], offset))
    real, imag = (real * cosine - imag * sine, real * sine + imag * cosine)
    real, imag = table_times(table(inner_ref), (real, imag), plain, -1)
    cosine, sine = (twist_back_ref[0], twist_back_ref[1])
    real, imag = (real * cosine + imag * sine, imag * cosine - real * sine)
    real, imag = table_times(
        table(outer_ref, slice(HALF_ROWS, ROWS)), (real, imag), turned, -1
    )
    real, imag = (real * (1.0 / NFFT), imag * (1.0 / NFFT))
    dedispersed_ref[0] = real.astype(jnp.bfloat16)
    dedispersed_ref[1] = imag.astype(jnp.bfloat16)
    power = real * real + imag * imag

    def exact_dot(a, b):
        return jnp.dot(a, b, precision=lax.Precision.HIGHEST, preferred_element_type=jnp.float32)

    def owner(shape, axis):
        rows = lax.broadcasted_iota(jnp.int32, shape, axis)
        windows = lax.broadcasted_iota(jnp.int32, shape, 1 - axis)
        return jnp.where(rows // WIN_ROWS == windows, 1.0, 0.0).astype(jnp.float32)

    gather = owner((WINDOWS, HALF_ROWS), 1)
    first_sum = jnp.sum(exact_dot(gather, power), axis=1, keepdims=True)
    second_sum = jnp.sum(exact_dot(gather, power * power), axis=1, keepdims=True)
    kurtosis = (
        (SKW + 1.0) / (SKW - 1.0) * (SKW * second_sum / (first_sum * first_sum + EPSILON) - 1.0)
    )
    scaled = (kurtosis - 1.0) / SK_WIDTH
    sk_weight = keep_ref[...] / (1.0 + scaled * scaled)
    sk_weight = jnp.broadcast_to(sk_weight, (WINDOWS, COLS))
    weight_ref[...] = sk_weight[:, :128]
    spread_weight = exact_dot(owner((HALF_ROWS, WINDOWS), 0), sk_weight)
    weighted_ref[...] = (spread_weight * power).astype(jnp.bfloat16).astype(jnp.float32)

    high_index = lax.broadcasted_iota(jnp.int32, (HIGH_BINS, LANES), 0)
    low_index = lax.broadcasted_iota(jnp.int32, (LOW_BINS, LANES), 0)

    def step(at, total):
        rows = pl.ds(pl.multiple_of(at * ROW_STEP, ROW_STEP), ROW_STEP)
        wide_rows = pl.ds(pl.multiple_of(at * 2 * ROW_STEP, 2 * ROW_STEP), 2 * ROW_STEP)
        bins, values = (bins_ref[wide_rows, :], weighted_ref[rows, :])
        high, low = (bins // LOW_BINS, bins % LOW_BINS)
        left, right = ([], [])
        for row in range(2 * ROW_STEP):
            value = values[row // 2 : row // 2 + 1, row % 2 * LANES : (row % 2 + 1) * LANES]
            left.append(
                jnp.where(high_index == high[row : row + 1], 1.0, 0.0).astype(jnp.bfloat16)
            )
            right.append(
                jnp.where(low_index == low[row : row + 1], value, 0.0).astype(jnp.bfloat16)
            )
        return total + lax.dot_general(
            jnp.concatenate(left, axis=1),
            jnp.concatenate(right, axis=1),
            (turned, ((), ())),
            preferred_element_type=jnp.float32,
        )

    total = lax.fori_loop(
        0, HALF_ROWS // ROW_STEP, step, jnp.zeros((HIGH_BINS, LOW_BINS), jnp.float32)
    )
    per_row = LANES // LOW_BINS
    total = jnp.concatenate([total, jnp.zeros((HIGH_BINS, LANES - LOW_BINS), jnp.float32)], axis=1)
    place = lax.broadcasted_iota(jnp.int32, (HIGH_BINS, LANES), 0) % per_row
    moved = jnp.where(place == 0, total, 0.0)
    for at in range(1, per_row):
        moved = moved + jnp.where(place == at, pltpu.roll(total, at * LOW_BINS, 1), 0.0)
    lines = BINS // LANES // shards
    for line in range(BINS // LANES):
        send_ref[line // lines, line % lines : line % lines + 1] = jnp.sum(
            moved[line * per_row : (line + 1) * per_row], axis=0, keepdims=True
        )
    pl.semaphore_wait(barrier, everyone - 1)

    def outgoing(index):
        return pltpu.make_async_remote_copy(
            src_ref=send_ref.at[lax.rem(index, shards)], dst_ref=recv_ref.at[here],
            send_sem=sems.at[0, index], recv_sem=sems.at[1, here],
            device_id=target(index), device_id_type=MESH,
        )

    def incoming(index):
        return pltpu.make_async_remote_copy(
            src_ref=send_ref.at[lax.rem(index, shards)], dst_ref=recv_ref.at[index],
            send_sem=sems.at[0, index], recv_sem=sems.at[1, index],
            device_id=target(index), device_id_type=MESH,
        )

    def begin(step, carry):
        outgoing(lax.rem(here + step, everyone)).start()
        return carry

    def arrive(step, carry):
        incoming(lax.rem(here + everyone - step, everyone)).wait_recv()
        return carry

    def leave(step, carry):
        outgoing(lax.rem(here + step, everyone)).wait_send()
        return carry

    lax.fori_loop(1, everyone, begin, 0)
    recv_ref[here] = send_ref[lax.axis_index("tm")]
    lax.fori_loop(1, everyone, arrive, 0)
    scale = BINS / (HALF_ROWS * COLS * shards)
    band = None
    mine = lax.axis_index("chan")
    for chan in range(chans):
        line = recv_ref[chan * shards]
        for at in range(1, shards):
            line = line + recv_ref[chan * shards + at]
        line = line * scale
        own = jnp.where(mine == chan, line, 0.0)
        band, profile = (line, own) if band is None else (band + line, profile + own)
    profile_ref[...] = profile
    band_ref[...] = band
    lax.fori_loop(1, everyone, leave, 0)


def fold(offset, wide, chirp, keep, bins, chans, shards):
    vmem = pl.BlockSpec(memory_space=pltpu.VMEM)
    tables = (dft_parts(ROWS), dft_parts(COLS), twiddle(ROWS, COLS), twiddle(COLS, ROWS))
    lines = BINS // LANES // shards
    line = jax.ShapeDtypeStruct((lines, LANES), jnp.float32)
    return pl.pallas_call(
        functools.partial(fold_kernel, chans, shards),
        out_shape=(
            jax.ShapeDtypeStruct((2, HALF_ROWS, COLS), jnp.bfloat16),
            jax.ShapeDtypeStruct((WINDOWS, 128), jnp.float32),
            line,
            line,
        ),
        in_specs=[pl.BlockSpec(memory_space=pltpu.SMEM)] + [vmem] * 8,
        out_specs=(vmem,) * 4,
        scratch_shapes=[
            pltpu.VMEM((HALF_ROWS, COLS), jnp.float32),
            pltpu.VMEM((shards, lines, LANES), jnp.float32),
            pltpu.VMEM((chans * shards, lines, LANES), jnp.float32),
            pltpu.SemaphoreType.DMA((2, chans * shards)),
        ],
        compiler_params=pltpu.CompilerParams(
            vmem_limit_bytes=40 << 20, collective_id=1, has_side_effects=True
        ),
        cost_estimate=pl.CostEstimate(
            flops=6 * 10**9, bytes_accessed=6 << 20, transcendentals=0
        ),
        name="fold",
    )(offset, wide, chirp, keep, bins, *[jnp.asarray(table) for table in tables])


def on_device(voltages, antenna_gains, chirp_phase, offsets, flags, sample_phase_bins):
    shards, chans = (lax.axis_size("tm"), lax.axis_size("chan"))
    antennas, channels, samples = voltages.shape[1:]
    assert channels == 1 and shards % 2 == 0
    volts = voltages.reshape(2, antennas, samples // LANES, LANES)
    volts = jnp.transpose(volts, (0, 2, 1, 3)).reshape(2, samples // LANES * antennas, LANES)
    gains = jnp.transpose(antenna_gains, (0, 2, 1))
    wide = beam(volts, gains, antennas, shards)
    chirp = chirp_phase.reshape(COLS, ROWS)
    keep = (1 - flags).astype(jnp.float32).reshape(WINDOWS, 1)
    bins = sample_phase_bins.reshape(-1, LANES)
    dedispersed, weight, profile, band = fold(offsets, wide, chirp, keep, bins, chans, shards)
    return (
        dedispersed.reshape(2, 1, HALF_ROWS * COLS),
        weight[:, 0].reshape(1, WINDOWS),
        profile.reshape(1, BINS // shards),
        band.reshape(BINS // shards),
    )


def solution(mesh):
    placed = (
        P(None, "tm", "chan", None),
        P(None, None, "chan"),
        P("chan", None),
        P("chan"),
        P("chan", "tm"),
        P("tm"),
    )
    return jax.shard_map(
        on_device,
        mesh=mesh,
        in_specs=placed,
        out_specs=(P(None, "chan", "tm"), P("chan", "tm"), P("chan", "tm"), P("tm")),
        check_vma=False,
    )
```

time: 130 us -> 56.8 us (0.44); the launches traced: 128 us -> 56.6 us
  blocking collectives: 42.9 us -> 0 us
  starting transfers between devices: 8.55 us -> 0 us
  Pallas kernels: 56.4 us -> 48.4 us
  local copies, waits for them, and re-layouts: 9.16 us -> 3.25 us
  waiting for transfers between devices: 3.32 us -> 0 us
  other arithmetic: 6.44 us -> 3.59 us
    all_to_all x1 -> x0, blocking collectives: 31.8 us -> none  [on_device(): pieces = lax.all_to_all(partial_beam, 'tm', 0, 0, tiled=True)]
    all_gather x1 -> x0, blocking collectives: 11.2 us -> none  [on_device(): lax.all_gather(jnp.sum(profile, axis=0), 'chan')]
    pallas_call x2, Pallas kernels: 56.4 us -> 48.4 us  [the longest x1 26.3 us: fold(): pl.pallas_call(functools.partial(fold_kernel, chans, shards), out_shape=(...]
    all_to_all x1 -> x0, starting transfers between devices: 5.17 us -> none  [on_device(): gathered = lax.all_to_all(blocks, 'tm', 0, 0, tiled=True)]
    ppermute x2 -> x0, starting transfers between devices: 3.38 us -> none  [shifted(): lax.ppermute(value, axis, [(source, source + steps) for source in range(f...]
    all_to_all x1 -> x0, waiting for transfers between devices: 3.31 us -> none  [on_device(): gathered = lax.all_to_all(blocks, 'tm', 0, 0, tiled=True)]
    reduce_sum x3 -> x0, other arithmetic: 2.48 us -> none  [the longest x1 1.87 us: on_device(): beam_sum = jnp.sum(pieces.astype(jnp.float32), axis=0)]
    unnamed x17 -> x15, local copies, waits for them, and re-layouts: 3.63 us -> 1.67 us
  transfers between devices with their start and end apart: 3 -> 0, of which waited for: 1 -> 0; matrix products, arithmetic and copies ran while one was open for 5% -> 0% of each run, Pallas kernels for 0% -> 0%
where the time goes in v1:
time: 56.8 us; the launch traced here: 56.6 us
  Pallas kernels  48.4 us (85%)
  other arithmetic  3.59 us (6%)
  local copies, waits for them, and re-layouts  3.25 us (6%)
  between operations  1.42 us (2%)
    pallas_call x1, Pallas kernels, fold(): pl.pallas_call(functools.partial(fold_kernel, chans, shards), out_shape=(...  26.3 us
    pallas_call x1, Pallas kernels, beam(): pl.pallas_call(functools.partial(beam_kernel, antennas, pairs), out_shape...  22.1 us
    unnamed x1, other arithmetic  2.93 us
    unnamed x15, local copies, waits for them, and re-layouts  1.67 us

profile of v1, /device:TPU:0, one launch (start us, length us, event | category | flops | bytes accessed | tf_op | source)
XLA Modules:
  0.0 56.6 jit_solution(1788766337827117453)
XLA Ops:
  0.6 0.0 copy-start
  1.3 0.7 %convert_bitcast_fusion = f32[64,1]{0,1:T(1,128)S(1)} fusion(s32[1,64]{1,0:T(1,128)} %param.14), kind=kLoop, calls=%fused_computation.1 | loop fusion | flops 128 | bytes 512 | tf_op jit(solution)/shard_map/reshape | solution.py:543
  2.0 0.1 copy.17.keep_ref
  2.1 0.5 broadcast.4
  2.6 2.9 %reduce.5 = f32[131072]{0:T(1024)S(1)} reduce(f32[1,131072]{1,0:T(1,128)} %param.12, f32[]{:T(128)} %broadcast.4), dimensions={0}, to_apply=%param.12.reduce_sub_computation.3 | reduce | bytes 1048580 | tf_op args[2]
  5.5 0.1 reshape.34.chirp_ref
  5.6 0.0 copy-done
  5.6 0.0 copy-start.1
  5.6 0.0 copy-start.2
  5.6 0.0 copy-start.3
  5.6 0.0 copy-start.4
  5.7 0.0 copy-start.5
  5.7 22.1 %beam.1.wide_ref = f32[2,528,256]{2,1,0:T(8,128)S(1)} custom-call(bf16[2,32768,128]{2,1,0:T(8,128)(2,1)} %bitcast.18, f32[2,1,64]{2,1,0:T(1,128)S(1)} %bitcast.14), custom_call_target="tpu_custom_call" | custom-call | flops 3000000000 | bytes 18874368 | tf_op jit(solution)/shard_map/beam/pallas_call | solution.py:319
  27.7 0.0 copy-done.1
  27.7 0.0 copy-done.2
  27.8 0.0 copy-done.3
  27.8 0.0 copy-done.4
  27.8 0.0 copy-done.5
  27.8 26.3 %fold.1 = (bf16[2,256,256]{2,1,0:T(8,128)(2,1)S(1)}, f32[64,128]{1,0:T(8,128)S(1)}, f32[2,128]{1,0:T(2,128)S(1)}, f32[2,128]{1,0:T(2,128)S(1)}) custom-call(s32[1]{0:T(128)S(6)} %copy.20.offset_ref, f32[2,528,256]{2,1,0:T(8,128)S(1)} %beam.1.wide_ref, f32[256,512]{1,0:T(8,128)S(1)} %reshape.34.chirp_ref, f32[64,1]{1,0:T(8,128)S(1)} %copy.17.keep_ref, ...), custom_call_target="tpu_custom_call" | custom-call | flops 6000000000 | bytes 6291456 | tf_op jit(solution)/shard_map/fold/pallas_call | solution.py:508
  54.1 0.8 %reshape.37 = bf16[2,1,65536]{2,0,1:T(2,128)(2,1)} reshape(bf16[2,256,256]{2,1,0:T(8,128)(2,1)S(1)} %get-tuple-element.8) | data formatting | bytes 524288 | tf_op jit(solution)/shard_map/reshape | solution.py:547
  54.9 0.6 %slice_reduce_fusion = f32[64]{0:T(128)} fusion(f32[64,128]{1,0:T(8,128)S(1)} %get-tuple-element.9), kind=kLoop, calls=%fused_computation | loop fusion | bytes 512 | tf_op jit(solution)/shard_map/slice | solution.py:548
  55.5 0.6 copy.21
  56.1 0.6 copy.22
Async XLA Ops:
  0.6 5.0 %copy-start = (f32[2,64,1]{1,2,0:T(1,128)S(1)}, f32[2,64,1]{1,2,0:T(1,128)}, u32[]{:S(2)}) copy-start(f32[2,64,1]{1,2,0:T(1,128)} %param.11) | copy-start | bytes 1540
  5.6 22.1 %copy-start.1 = (s32[65536]{0:T(1024)S(1)}, s32[65536]{0:T(1024)}, u32[]{:S(2)}) copy-start(s32[65536]{0:T(1024)} %param.15) | copy-start | bytes 786436
  5.6 22.1 %copy-start.2 = (bf16[2,2,512,512]{3,2,1,0:T(8,128)(2,1)S(1)}, bf16[2,2,512,512]{3,2,1,0:T(8,128)(2,1)}, u32[]{:S(2)}) copy-start(bf16[2,2,512,512]{3,2,1,0:T(8,128)(2,1)} %constant.10.clone.outer_ref) | copy-start | bytes 6291460
  5.6 22.1 %copy-start.3 = (f32[2,256,512]{2,1,0:T(8,128)S(1)}, f32[2,256,512]{2,1,0:T(8,128)}, u32[]{:S(2)}) copy-start(f32[2,256,512]{2,1,0:T(8,128)} %constant.13.clone.twist_back_ref) | copy-start | bytes 3145732
  5.6 22.1 %copy-start.4 = (f32[2,512,256]{2,1,0:T(8,128)S(1)}, f32[2,512,256]{2,1,0:T(8,128)}, u32[]{:S(2)}) copy-start(f32[2,512,256]{2,1,0:T(8,128)} %constant.12.clone.twist_ref) | copy-start | bytes 3145732
  5.7 22.1 %copy-start.5 = (bf16[2,2,256,256]{3,2,1,0:T(8,128)(2,1)S(1)}, bf16[2,2,256,256]{3,2,1,0:T(8,128)(2,1)}, u32[]{:S(2)}) copy-start(bf16[2,2,256,256]{3,2,1,0:T(8,128)(2,1)} %constant.11.clone.inner_ref) | copy-start | bytes 1572868

commit v2 on v1

--- a/solution.py
+++ b/solution.py
@@ -26,7 +26,8 @@
 WINDOWS = HALF_ROWS // WIN_ROWS
 LOW_BINS = 32
 HIGH_BINS = BINS // LOW_BINS
-ROW_STEP = 8
+BLOCK_ROWS = 128
+STEP_LINES = 32
 LANES = 128
 DEPTH = 256
 PARTS = 4
@@ -40,17 +41,26 @@
     return np.stack([high, low])
 
 
-def dft_parts(length):
-    index = np.arange(length, dtype=np.int64)
-    angle = -2.0 * math.pi / length * (index[:, None] * index[None, :] % length)
-    real, imag = (np.cos(angle).astype(np.float32), np.sin(angle).astype(np.float32))
-    return np.stack([bf16_split(real), bf16_split(imag)])
-
-
-def twiddle(row_total, col_total):
-    turns = np.arange(row_total, dtype=np.int64)[:, None] * np.arange(col_total, dtype=np.int64) % NFFT
-    angle = -2.0 * math.pi / NFFT * turns
-    return np.stack([np.cos(angle), np.sin(angle)]).astype(np.float32)
+def unit_roots(turns, period):
+    angle = -2.0 * math.pi / period * (turns % period)
+    return (np.cos(angle).astype(np.float32), np.sin(angle).astype(np.float32))
+
+
+def dft_table():
+    index = np.arange(COLS, dtype=np.int64)
+    real, imag = unit_roots(index[:, None] * index[None, :], COLS)
+    return np.stack([bf16_split(real), bf16_split(imag), bf16_split(-imag)])
+
+
+def twiddle():
+    index = np.arange(HALF_ROWS, dtype=np.int64)
+    rows = np.stack([2 * index, 2 * index + 1])
+    return np.stack(unit_roots(rows[:, :, None] * np.arange(COLS, dtype=np.int64), NFFT))
+
+
+def half_turns():
+    index = np.arange(HALF_ROWS, dtype=np.int64)
+    return np.stack(unit_roots(np.repeat(index[:, None], LANES, axis=1), ROWS))
 
 
 def split(value):
@@ -58,22 +68,16 @@
     return high, (value - high.astype(jnp.float32)).astype(jnp.bfloat16)
 
 
-def three_pass(left, right, dims):
-    def product(a, b):
-        return lax.dot_general(a, b, (dims, ((), ())), preferred_element_type=jnp.float32)
-
-    return product(left[0], right[0]) + (product(left[0], right[1]) + product(left[1], right[0]))
-
-
-def table_times(table, pair, dims, sign):
-    real, imag = (split(pair[0]), split(pair[1]))
-    rr = three_pass(table[0], real, dims)
-    ii = three_pass(table[1], imag, dims)
-    ri = three_pass(table[0], imag, dims)
-    ir = three_pass(table[1], real, dims)
-    if sign > 0:
-        return rr - ii, ri + ir
-    return rr + ii, ri - ir
+def product(*pairs):
+    left, right = ([], [])
+    for a, b in pairs:
+        left += [a[0], a[0], a[1]]
+        right += [b[0], b[1], b[0]]
+    return jnp.dot(
+        jnp.concatenate(left, axis=1),
+        jnp.concatenate(right, axis=0),
+        preferred_element_type=jnp.float32,
+    )
 
 
 def cos_sin(angle):
@@ -89,14 +93,16 @@
     return 1.0 - 2.0 * sine * sine, 2.0 * sine * cosine
 
 
-def shifted_phase(phase, offset):
-    high = lax.broadcasted_iota(jnp.int32, phase.shape, 0) * ROWS
-    index = high + lax.broadcasted_iota(jnp.int32, phase.shape, 1)
+def response(phase, first, first_column, offset):
+    index = first + lax.broadcasted_iota(jnp.int32, phase.shape, 0)
+    column = first_column + lax.broadcasted_iota(jnp.int32, phase.shape, 1)
+    index = index + ROWS * column
     turns = (index * offset) & (NFFT - 1)
     turns = jnp.where(turns >= NFFT // 2, turns - NFFT, turns)
     phase = phase + turns.astype(jnp.float32) * (2.0 * math.pi / NFFT)
     phase = jnp.where(phase > math.pi, phase - 2.0 * math.pi, phase)
-    return jnp.where(phase < -math.pi, phase + 2.0 * math.pi, phase)
+    phase = jnp.where(phase < -math.pi, phase + 2.0 * math.pi, phase)
+    return cos_sin(phase)
 
 
 def weight_table(gains_ref, table_ref, antennas, me):
@@ -154,9 +160,10 @@
 
 
 def beam_kernel(
-    antennas, pairs, volt_ref, gains_ref, wide_ref, table_ref, vbuf, pair_send, pair_recv,
-    chip_send, chip_recv, own_ref, halo_ref, head_ref, load_sem, pair_sems, chip_sems, halo_sems,
-    head_sems,
+    antennas, pairs, volt_ref, gains_ref, offset_ref, chirp_hbm, turns_hbm, data_ref, response_ref,
+    table_ref, vbuf, pair_send, pair_recv, chip_send, chip_recv, own_ref, halo_send, halo_ref,
+    head_ref, chirp_ref, turns_ref, block_ref, load_sem, pair_sems, chip_sems, halo_sems,
+    head_sems, side_sems,
 ):
     count = 2 * pairs
     me = lax.axis_index("tm")
@@ -187,6 +194,13 @@
         return carry
 
     lax.fori_loop(0, PARTS, begin, 0)
+    side = [
+        pltpu.make_async_copy(chirp_hbm, chirp_ref, side_sems.at[0]),
+        pltpu.make_async_copy(turns_hbm, turns_ref, side_sems.at[1]),
+    ]
+    for copy in side:
+        copy.start()
+    offset = offset_ref[0]
     weight_table(gains_ref, table_ref, antennas, me)
 
     def pair_copy(part, j):
@@ -205,14 +219,14 @@
 
     def halo_copy(part):
         return pltpu.make_async_remote_copy(
-            src_ref=own_ref.at[part], dst_ref=halo_ref.at[part],
+            src_ref=halo_send.at[part], dst_ref=halo_ref.at[part],
             send_sem=halo_sems.at[0, part], recv_sem=halo_sems.at[1, part],
             device_id={"tm": lax.rem(me + 1, count)}, device_id_type=MESH,
         )
 
     def head_copy():
         return pltpu.make_async_remote_copy(
-            src_ref=own_ref.at[0, :, 0:HALO_ROWS], dst_ref=head_ref,
+            src_ref=halo_send.at[0, :, 0:HALO_ROWS], dst_ref=head_ref,
             send_sem=head_sems.at[0], recv_sem=head_sems.at[1],
             device_id={"tm": lax.rem(me + count - 1, count)}, device_id_type=MESH,
         )
@@ -224,12 +238,47 @@
         for j in range(pairs - 1):
             total = total + chip_recv[part, j].astype(jnp.float32)
         own_ref[part] = total
-        rows = pl.ds(pl.multiple_of(HALF_ROWS + part * PART_ROWS, PART_ROWS), PART_ROWS)
-        wide_ref[:, rows] = total
+        halo_send[part] = total.astype(jnp.bfloat16)
 
         @pl.when(me < count - 1)
         def _():
             halo_copy(part).start()
+
+    def chirp_block(at):
+        stride = ROWS // LANES
+        for half in range(COLS // LANES):
+            columns = chirp_ref[
+                pl.ds(at + half * LANES * stride, LANES, stride=stride), :
+            ]
+            phase = jnp.transpose(columns, (1, 0))
+            for out, value in enumerate(response(phase, at * LANES, half * LANES, offset)):
+                block_ref[...] = value * (1.0 / NFFT)
+                for parity in range(2):
+                    rows = pl.ds(pl.multiple_of(at * (LANES // 2), LANES // 2), LANES // 2)
+                    response_ref[out, parity, rows, half * LANES : (half + 1) * LANES] = (
+                        block_ref[pl.ds(parity, LANES // 2, stride=2), :]
+                    )
+
+    def combine(part, first=None):
+        rows = slice(part * PART_ROWS, (part + 1) * PART_ROWS)
+        before = [halo_ref[part, out].astype(jnp.float32) for out in range(2)]
+        if first is not None:
+            before = [
+                jnp.concatenate([head, value[HALO_ROWS:]], axis=0)
+                for head, value in zip(first, before)
+            ]
+        after = [own_ref[part, 0], own_ref[part, 1]]
+        real, imag = (before[0] - after[0], before[1] - after[1])
+        cosine, sine = [
+            jnp.concatenate([turns_ref[out, rows]] * (COLS // LANES), axis=1) for out in range(2)
+        ]
+        both = (
+            (before[0] + after[0], before[1] + after[1]),
+            (real * cosine - imag * sine, real * sine + imag * cosine),
+        )
+        for kind, values in enumerate(both):
+            for out, value in enumerate(values):
+                data_ref[kind, out, 0, rows], data_ref[kind, out, 1, rows] = split(value)
 
     def run(part, carry):
         for j in range(pairs):
@@ -265,6 +314,13 @@
             if j < pairs - 1:
                 chip_copy(part, j).start()
 
+        @pl.when(part == 0)
+        def _():
+            for copy in side:
+                copy.wait()
+
+        chirp_block(part)
+
         @pl.when(part > 0)
         def _():
             finish(part - 1)
@@ -278,27 +334,47 @@
     lax.fori_loop(0, PARTS, run, 0)
     finish(PARTS - 1)
 
+    @pl.when(me == 0)
+    def _():
+        halo_ref[...] = jnp.zeros((PARTS, 2, PART_ROWS, COLS), jnp.bfloat16)
+
+    @pl.when(me == count - 1)
+    def _():
+        head_ref[...] = jnp.zeros((2, HALO_ROWS, COLS), jnp.bfloat16)
+
+    for part in range(PARTS):
+
+        @pl.when(me > 0)
+        def _():
+            halo_copy(part).wait_recv()
+
+        first = None
+        if part == 0:
+
+            @pl.when(me < count - 1)
+            def _():
+                head_copy().wait_recv()
+
+            spot = lax.broadcasted_iota(jnp.int32, (HALO_ROWS, COLS), 0) * COLS
+            spot = spot + lax.broadcasted_iota(jnp.int32, (HALO_ROWS, COLS), 1)
+            first = [
+                jnp.where(
+                    spot < offset,
+                    head_ref[out].astype(jnp.float32),
+                    halo_ref[0, out, 0:HALO_ROWS].astype(jnp.float32),
+                )
+                for out in range(2)
+            ]
+        combine(part, first)
+
     @pl.when(me > 0)
     def _():
-        for part in range(PARTS):
-            halo_copy(part).wait_recv()
-            wide_ref[:, part * PART_ROWS : (part + 1) * PART_ROWS] = halo_ref[part]
         head_copy().wait_send()
-
-    @pl.when(me == 0)
-    def _():
-        wide_ref[:, 0:HALF_ROWS] = jnp.zeros((2, HALF_ROWS, COLS), jnp.float32)
 
     @pl.when(me < count - 1)
     def _():
-        head_copy().wait_recv()
-        wide_ref[:, ROWS : ROWS + HALO_ROWS] = head_ref[...]
         for part in range(PARTS):
             halo_copy(part).wait_send()
-
-    @pl.when(me == count - 1)
-    def _():
-        wide_ref[:, ROWS : ROWS + HALO_ROWS] = jnp.zeros((2, HALO_ROWS, COLS), jnp.float32)
 
     def drain(part, carry):
         for j in range(pairs):
@@ -310,17 +386,22 @@
     lax.fori_loop(0, PARTS, drain, 0)
 
 
-def beam(volts, gains, antennas, shards):
+def beam(volts, gains, offset, chirp, shards):
     pairs = shards // 2
     size = volts.shape[1] // shards // PARTS
+    antennas = size * LANES // (PART_ROWS * COLS)
     half = DEPTH // antennas // 2
     block = (2, PART_ROWS, COLS)
     vmem = pl.BlockSpec(memory_space=pltpu.VMEM)
+    hbm = pl.BlockSpec(memory_space=pl.ANY)
     return pl.pallas_call(
         functools.partial(beam_kernel, antennas, pairs),
-        out_shape=jax.ShapeDtypeStruct((2, ROWS + HALO_ROWS, COLS), jnp.float32),
-        in_specs=[pl.BlockSpec(memory_space=pl.ANY), vmem],
-        out_specs=vmem,
+        out_shape=(
+            jax.ShapeDtypeStruct((2, 2, 2, HALF_ROWS, COLS), jnp.bfloat16),
+            jax.ShapeDtypeStruct((2, 2, HALF_ROWS, COLS), jnp.float32),
+        ),
+        in_specs=[hbm, vmem, pl.BlockSpec(memory_space=pltpu.SMEM), hbm, hbm],
+        out_specs=(vmem, vmem),
         scratch_shapes=[
             pltpu.VMEM((2, 8 * half, DEPTH), jnp.bfloat16),
             pltpu.VMEM((PARTS, shards, 2, size, LANES), jnp.bfloat16),
@@ -329,28 +410,33 @@
             pltpu.VMEM((PARTS, pairs - 1) + block, jnp.bfloat16),
             pltpu.VMEM((PARTS, pairs - 1) + block, jnp.bfloat16),
             pltpu.VMEM((PARTS,) + block, jnp.float32),
-            pltpu.VMEM((PARTS,) + block, jnp.float32),
-            pltpu.VMEM((2, HALO_ROWS, COLS), jnp.float32),
+            pltpu.VMEM((PARTS,) + block, jnp.bfloat16),
+            pltpu.VMEM((PARTS,) + block, jnp.bfloat16),
+            pltpu.VMEM((2, HALO_ROWS, COLS), jnp.bfloat16),
+            pltpu.VMEM((NFFT // LANES, LANES), jnp.float32),
+            pltpu.VMEM((2, HALF_ROWS, LANES), jnp.float32),
+            pltpu.VMEM((LANES, LANES), jnp.float32),
             pltpu.SemaphoreType.DMA((PARTS, shards)),
             pltpu.SemaphoreType.DMA((2, PARTS, pairs)),
             pltpu.SemaphoreType.DMA((2, PARTS, pairs - 1)),
             pltpu.SemaphoreType.DMA((2, PARTS)),
             pltpu.SemaphoreType.DMA((2,)),
+            pltpu.SemaphoreType.DMA((2,)),
         ],
         compiler_params=pltpu.CompilerParams(
-            vmem_limit_bytes=40 << 20, collective_id=0, has_side_effects=True
+            vmem_limit_bytes=44 << 20, collective_id=0, has_side_effects=True
         ),
         cost_estimate=pl.CostEstimate(
             flops=3 * 10**9, bytes_accessed=18 << 20, transcendentals=0
         ),
         name="beam",
-    )(volts, gains)
+    )(volts, gains, offset, chirp, jnp.asarray(half_turns()))
 
 
 def fold_kernel(
-    chans, shards, offset_ref, wide_ref, chirp_ref, keep_ref, bins_ref, outer_ref, inner_ref,
-    twist_ref, twist_back_ref, dedispersed_ref, weight_ref, profile_ref, band_ref, weighted_ref,
-    send_ref, recv_ref, sems,
+    chans, shards, data_ref, response_ref, flags_ref, bins_ref, dft_ref, twist_ref, turns_ref,
+    dedispersed_ref, small_ref, back_ref, weighted_ref, high_ref, low_ref, send_ref, recv_ref,
+    sems,
 ):
     everyone = chans * shards
     here = lax.axis_index("chan") * shards + lax.axis_index("tm")
@@ -366,83 +452,131 @@
         return carry
 
     lax.fori_loop(1, everyone, greet, 0)
-    offset = offset_ref[0]
-    spot = lax.broadcasted_iota(jnp.int32, (HALO_ROWS, COLS), 0) * COLS
-    spot = spot + lax.broadcasted_iota(jnp.int32, (HALO_ROWS, COLS), 1)
-    signal = []
-    for half in range(2):
-        first = jnp.where(spot < offset, wide_ref[half, ROWS:], wide_ref[half, :HALO_ROWS])
-        signal.append(jnp.concatenate([first, wide_ref[half, HALO_ROWS:ROWS]], axis=0))
-
-    def table(ref, rows=slice(None)):
-        return [[ref[0, 0, rows], ref[0, 1, rows]], [ref[1, 0, rows], ref[1, 1, rows]]]
-
-    plain, turned = (((1,), (0,)), ((1,), (1,)))
-    real, imag = table_times(table(outer_ref), signal, plain, 1)
-    cosine, sine = (twist_ref[0], twist_ref[1])
-    real, imag = (real * cosine - imag * sine, real * sine + imag * cosine)
-    real, imag = table_times(table(inner_ref), (real, imag), turned, 1)
-    cosine, sine = cos_sin(shifted_phase(chirp_ref[...], offset))
-    real, imag = (real * cosine - imag * sine, real * sine + imag * cosine)
-    real, imag = table_times(table(inner_ref), (real, imag), plain, -1)
-    cosine, sine = (twist_back_ref[0], twist_back_ref[1])
-    real, imag = (real * cosine + imag * sine, imag * cosine - real * sine)
-    real, imag = table_times(
-        table(outer_ref, slice(HALF_ROWS, ROWS)), (real, imag), turned, -1
-    )
-    real, imag = (real * (1.0 / NFFT), imag * (1.0 / NFFT))
-    dedispersed_ref[0] = real.astype(jnp.bfloat16)
-    dedispersed_ref[1] = imag.astype(jnp.bfloat16)
-    power = real * real + imag * imag
-
-    def exact_dot(a, b):
-        return jnp.dot(a, b, precision=lax.Precision.HIGHEST, preferred_element_type=jnp.float32)
-
-    def owner(shape, axis):
-        rows = lax.broadcasted_iota(jnp.int32, shape, axis)
-        windows = lax.broadcasted_iota(jnp.int32, shape, 1 - axis)
-        return jnp.where(rows // WIN_ROWS == windows, 1.0, 0.0).astype(jnp.float32)
-
-    gather = owner((WINDOWS, HALF_ROWS), 1)
-    first_sum = jnp.sum(exact_dot(gather, power), axis=1, keepdims=True)
-    second_sum = jnp.sum(exact_dot(gather, power * power), axis=1, keepdims=True)
-    kurtosis = (
-        (SKW + 1.0) / (SKW - 1.0) * (SKW * second_sum / (first_sum * first_sum + EPSILON) - 1.0)
-    )
-    scaled = (kurtosis - 1.0) / SK_WIDTH
-    sk_weight = keep_ref[...] / (1.0 + scaled * scaled)
-    sk_weight = jnp.broadcast_to(sk_weight, (WINDOWS, COLS))
-    weight_ref[...] = sk_weight[:, :128]
-    spread_weight = exact_dot(owner((HALF_ROWS, WINDOWS), 0), sk_weight)
-    weighted_ref[...] = (spread_weight * power).astype(jnp.bfloat16).astype(jnp.float32)
-
+    def table(at):
+        return (dft_ref[at, 0], dft_ref[at, 1])
+
+    real_table, imag_table, minus_table = (table(0), table(1), table(2))
+
+    def ahead(tables, at):
+        return tuple(half[at] for half in tables)
+
+    for kind in range(2):
+        given = [(data_ref[kind, out, 0], data_ref[kind, out, 1]) for out in range(2)]
+        for start in range(0, HALF_ROWS, BLOCK_ROWS):
+            rows = slice(start, start + BLOCK_ROWS)
+            left, cross, minus = (
+                ahead(real_table, rows), ahead(imag_table, rows), ahead(minus_table, rows)
+            )
+            real = product((left, given[0]), (minus, given[1]))
+            imag = product((left, given[1]), (cross, given[0]))
+            cosine, sine = (twist_ref[0, kind, rows], twist_ref[1, kind, rows])
+            pair = (split(real * cosine - imag * sine), split(real * sine + imag * cosine))
+            real = product((pair[0], real_table), (pair[1], minus_table))
+            imag = product((pair[0], imag_table), (pair[1], real_table))
+            turn, tilt = (response_ref[0, kind, rows], response_ref[1, kind, rows])
+            pair = (split(real * turn - imag * tilt), split(real * tilt + imag * turn))
+            real = product((pair[0], real_table), (pair[1], imag_table))
+            imag = product((pair[0], minus_table), (pair[1], real_table))
+            for out, value in enumerate(
+                (real * cosine + imag * sine, imag * cosine - real * sine)
+            ):
+                back_ref[kind, out, 0, rows], back_ref[kind, out, 1, rows] = split(value)
+
+    flag = flags_ref[...]
+    if WINDOWS < LANES:
+        flag = jnp.concatenate([flag, jnp.zeros((1, LANES - WINDOWS), jnp.int32)], axis=1)
+    keep_row = (1 - flag).astype(jnp.float32)
+    shape = (BLOCK_ROWS, LANES)
+    row_index = lax.broadcasted_iota(jnp.int32, shape, 0)
+    lane_index = lax.broadcasted_iota(jnp.int32, shape, 1)
+
+    def window_sum(values):
+        total = jnp.broadcast_to(jnp.sum(values, axis=1, keepdims=True), shape)
+        reach = 1
+        while reach < WIN_ROWS:
+            up, down = (pltpu.roll(total, BLOCK_ROWS - reach, 0), pltpu.roll(total, reach, 0))
+            total = total + jnp.where(row_index % (2 * reach) < reach, up, down)
+            reach *= 2
+        return total
+
+    per_line = COLS // LANES
+    weight_row = jnp.zeros((1, LANES), jnp.float32)
+    for start in range(0, HALF_ROWS, BLOCK_ROWS):
+        rows = slice(start, start + BLOCK_ROWS)
+        left, cross, minus = (
+            ahead(real_table, rows), ahead(imag_table, rows), ahead(minus_table, rows)
+        )
+        parts = []
+        for kind in range(2):
+            given = [(back_ref[kind, out, 0], back_ref[kind, out, 1]) for out in range(2)]
+            parts.append(
+                (
+                    product((left, given[0]), (cross, given[1])),
+                    product((left, given[1]), (minus, given[0])),
+                )
+            )
+        cosine, sine = [
+            jnp.concatenate([turns_ref[out, rows]] * (COLS // LANES), axis=1) for out in range(2)
+        ]
+        (real, imag), (odd_real, odd_imag) = parts
+        real = real - (odd_real * cosine + odd_imag * sine)
+        imag = imag - (odd_imag * cosine - odd_real * sine)
+        dedispersed_ref[0, rows] = real.astype(jnp.bfloat16)
+        dedispersed_ref[1, rows] = imag.astype(jnp.bfloat16)
+        power = real * real + imag * imag
+        first_sum, second_sum = (window_sum(power), window_sum(power * power))
+        kurtosis = (
+            (SKW + 1.0)
+            / (SKW - 1.0)
+            * (SKW * second_sum / (first_sum * first_sum + EPSILON) - 1.0)
+        )
+        scaled = (kurtosis - 1.0) / SK_WIDTH
+        window = (row_index + start) // WIN_ROWS
+        keep = jnp.where(lane_index == window, jnp.broadcast_to(keep_row, shape), 0.0)
+        keep = jnp.sum(keep, axis=1, keepdims=True)
+        sk_weight = keep / (1.0 + scaled * scaled)
+        chosen = (row_index + start) == lane_index * WIN_ROWS
+        weight_row = weight_row + jnp.sum(
+            jnp.where(chosen, sk_weight, 0.0), axis=0, keepdims=True
+        )
+        for at in range(COLS // LANES):
+            lanes = slice(at * LANES, (at + 1) * LANES)
+            value = (sk_weight * power[:, lanes]).astype(jnp.bfloat16)
+            places = pl.ds(start * per_line + at, BLOCK_ROWS, stride=per_line)
+            weighted_ref[places, :] = value.astype(jnp.float32)
+
+    bins = bins_ref[...]
+    high_ref[...] = (bins // LOW_BINS).astype(jnp.float32)
+    low_ref[...] = (bins % LOW_BINS).astype(jnp.float32)
     high_index = lax.broadcasted_iota(jnp.int32, (HIGH_BINS, LANES), 0)
+    high_index = high_index.astype(jnp.float32).astype(jnp.bfloat16)
     low_index = lax.broadcasted_iota(jnp.int32, (LOW_BINS, LANES), 0)
+    low_index = low_index.astype(jnp.float32).astype(jnp.bfloat16)
+    one, zero = (jnp.bfloat16(1.0), jnp.bfloat16(0.0))
 
     def step(at, total):
-        rows = pl.ds(pl.multiple_of(at * ROW_STEP, ROW_STEP), ROW_STEP)
-        wide_rows = pl.ds(pl.multiple_of(at * 2 * ROW_STEP, 2 * ROW_STEP), 2 * ROW_STEP)
-        bins, values = (bins_ref[wide_rows, :], weighted_ref[rows, :])
-        high, low = (bins // LOW_BINS, bins % LOW_BINS)
+        start = at * STEP_LINES
         left, right = ([], [])
-        for row in range(2 * ROW_STEP):
-            value = values[row // 2 : row // 2 + 1, row % 2 * LANES : (row % 2 + 1) * LANES]
-            left.append(
-                jnp.where(high_index == high[row : row + 1], 1.0, 0.0).astype(jnp.bfloat16)
-            )
-            right.append(
-                jnp.where(low_index == low[row : row + 1], value, 0.0).astype(jnp.bfloat16)
-            )
+
+        def spread(block, line, count):
+            return jnp.broadcast_to(block[line : line + 1], (count, LANES)).astype(jnp.bfloat16)
+
+        lines_here = pl.ds(start, STEP_LINES)
+        highs, lows, values = (high_ref[lines_here], low_ref[lines_here], weighted_ref[lines_here])
+        for line in range(STEP_LINES):
+            left.append(jnp.where(high_index == spread(highs, line, HIGH_BINS), one, zero))
+            value = spread(values, line, LOW_BINS)
+            right.append(jnp.where(low_index == spread(lows, line, LOW_BINS), value, zero))
         return total + lax.dot_general(
             jnp.concatenate(left, axis=1),
             jnp.concatenate(right, axis=1),
-            (turned, ((), ())),
+            ((((1,), (1,))), ((), ())),
             preferred_element_type=jnp.float32,
         )
 
-    total = lax.fori_loop(
-        0, HALF_ROWS // ROW_STEP, step, jnp.zeros((HIGH_BINS, LOW_BINS), jnp.float32)
-    )
+    total = jnp.zeros((HIGH_BINS, LOW_BINS), jnp.float32)
+    for at in range(HALF_ROWS * per_line // STEP_LINES):
+        total = step(at, total)
     per_row = LANES // LOW_BINS
     total = jnp.concatenate([total, jnp.zeros((HIGH_BINS, LANES - LOW_BINS), jnp.float32)], axis=1)
     place = lax.broadcasted_iota(jnp.int32, (HIGH_BINS, LANES), 0) % per_row
@@ -495,28 +629,29 @@
         line = line * scale
         own = jnp.where(mine == chan, line, 0.0)
         band, profile = (line, own) if band is None else (band + line, profile + own)
-    profile_ref[...] = profile
-    band_ref[...] = band
+    small_ref[0:lines] = profile
+    small_ref[lines : 2 * lines] = band
+    small_ref[2 * lines : 2 * lines + 1] = weight_row
     lax.fori_loop(1, everyone, leave, 0)
 
 
-def fold(offset, wide, chirp, keep, bins, chans, shards):
+def fold(data, reply, flags, bins, chans, shards):
     vmem = pl.BlockSpec(memory_space=pltpu.VMEM)
-    tables = (dft_parts(ROWS), dft_parts(COLS), twiddle(ROWS, COLS), twiddle(COLS, ROWS))
+    tables = (dft_table(), twiddle(), half_turns())
     lines = BINS // LANES // shards
-    line = jax.ShapeDtypeStruct((lines, LANES), jnp.float32)
     return pl.pallas_call(
         functools.partial(fold_kernel, chans, shards),
         out_shape=(
             jax.ShapeDtypeStruct((2, HALF_ROWS, COLS), jnp.bfloat16),
-            jax.ShapeDtypeStruct((WINDOWS, 128), jnp.float32),
-            line,
-            line,
+            jax.ShapeDtypeStruct((2 * lines + 1, LANES), jnp.float32),
         ),
-        in_specs=[pl.BlockSpec(memory_space=pltpu.SMEM)] + [vmem] * 8,
-        out_specs=(vmem,) * 4,
+        in_specs=[vmem] * 7,
+        out_specs=(vmem,) * 2,
         scratch_shapes=[
-            pltpu.VMEM((HALF_ROWS, COLS), jnp.float32),
+            pltpu.VMEM((2, 2, 2, HALF_ROWS, COLS), jnp.bfloat16),
+            pltpu.VMEM((HALF_ROWS * COLS // LANES, LANES), jnp.float32),
+            pltpu.VMEM((HALF_ROWS * COLS // LANES, LANES), jnp.float32),
+            pltpu.VMEM((HALF_ROWS * COLS // LANES, LANES), jnp.float32),
             pltpu.VMEM((shards, lines, LANES), jnp.float32),
             pltpu.VMEM((chans * shards, lines, LANES), jnp.float32),
             pltpu.SemaphoreType.DMA((2, chans * shards)),
@@ -528,7 +663,7 @@
             flops=6 * 10**9, bytes_accessed=6 << 20, transcendentals=0
         ),
         name="fold",
-    )(offset, wide, chirp, keep, bins, *[jnp.asarray(table) for table in tables])
+    )(data, reply, flags, bins, *[jnp.asarray(table) for table in tables])
 
 
 def on_device(voltages, antenna_gains, chirp_phase, offsets, flags, sample_phase_bins):
@@ -538,16 +673,15 @@
     volts = voltages.reshape(2, antennas, samples // LANES, LANES)
     volts = jnp.transpose(volts, (0, 2, 1, 3)).reshape(2, samples // LANES * antennas, LANES)
     gains = jnp.transpose(antenna_gains, (0, 2, 1))
-    wide = beam(volts, gains, antennas, shards)
-    chirp = chirp_phase.reshape(COLS, ROWS)
-    keep = (1 - flags).astype(jnp.float32).reshape(WINDOWS, 1)
+    data, reply = beam(volts, gains, offsets, chirp_phase.reshape(-1, LANES), shards)
     bins = sample_phase_bins.reshape(-1, LANES)
-    dedispersed, weight, profile, band = fold(offsets, wide, chirp, keep, bins, chans, shards)
+    dedispersed, small = fold(data, reply, flags, bins, chans, shards)
+    lines = BINS // LANES // shards
     return (
         dedispersed.reshape(2, 1, HALF_ROWS * COLS),
-        weight[:, 0].reshape(1, WINDOWS),
-        profile.reshape(1, BINS // shards),
-        band.reshape(BINS // shards),
+        small[2 * lines : 2 * lines + 1, :WINDOWS],
+        small[:lines].reshape(1, BINS // shards),
+        small[lines : 2 * lines].reshape(BINS // shards),
     )
 
 

time: 56.8 us -> 49.5 us (0.87)
  Pallas kernels: 48.4 us -> 43.4 us
  other arithmetic: 3.59 us -> 0 us
  local copies, waits for them, and re-layouts: 3.25 us -> 4.54 us
    pallas_call x1, Pallas kernels: 26.3 us -> 21.3 us  [fold(): pl.pallas_call(functools.partial(fold_kernel, chans, shards), out_shape=(...]
    unnamed x1 -> x0, other arithmetic: 2.93 us -> none
    unnamed x15 -> x16, local copies, waits for them, and re-layouts: 1.67 us -> 2.68 us
    reshape x1 -> x0, other arithmetic: 0.66 us -> none  [on_device(): keep = (1 - flags).astype(jnp.float32).reshape(WINDOWS, 1)]
where the time goes in v2:
time: 49.5 us; the launch traced here: 49.3 us
  Pallas kernels  43.4 us (88%)
  local copies, waits for them, and re-layouts  4.54 us (9%)
  between operations  1.37 us (3%)
    pallas_call x1, Pallas kernels, beam(): pl.pallas_call(functools.partial(beam_kernel, antennas, pairs), out_shape...  22.1 us
    pallas_call x1, Pallas kernels, fold(): pl.pallas_call(functools.partial(fold_kernel, chans, shards), out_shape=(...  21.3 us
    unnamed x16, local copies, waits for them, and re-layouts  2.68 us

profile of v2, /device:TPU:0, one launch (start us, length us, event | category | flops | bytes accessed | tf_op | source)
XLA Modules:
  0.0 49.3 jit_solution(17934768449111416062)
XLA Ops:
  0.6 0.0 copy-start.5
  1.3 0.0 copy-start
  1.3 1.0 %copy-done = f32[1,131072]{1,0:T(1,128)S(1)} copy-done((f32[1,131072]{1,0:T(1,128)S(1)}, f32[1,131072]{1,0:T(1,128)}, u32[]{:S(2)}) %copy-start) | copy-done | bytes 524312
  2.3 0.0 copy-start.1
  2.3 0.9 %copy-done.1 = f32[2,256,128]{2,1,0:T(8,128)S(1)} copy-done((f32[2,256,128]{2,1,0:T(8,128)S(1)}, f32[2,256,128]{2,1,0:T(8,128)}, u32[]{:S(2)}) %copy-start.1) | copy-done | bytes 262168
  3.3 0.0 copy-start.3
  3.3 0.7 %copy-done.3 = f32[2,64,1]{1,2,0:T(1,128)S(1)} copy-done((f32[2,64,1]{1,2,0:T(1,128)S(1)}, f32[2,64,1]{1,2,0:T(1,128)}, u32[]{:S(2)}) %copy-start.3) | copy-done | bytes 536
  4.0 0.0 copy-start.2
  4.0 0.0 copy-start.4
  4.0 0.0 copy-start.6
  4.0 0.0 copy-start.7
  4.0 22.1 %beam.1 = (bf16[2,2,2,256,256]{4,3,2,1,0:T(8,128)(2,1)S(1)}, f32[2,2,256,256]{3,2,1,0:T(8,128)S(1)}) custom-call(bf16[2,32768,128]{2,1,0:T(8,128)(2,1)} %bitcast.16, f32[2,1,64]{2,1,0:T(1,128)S(1)} %bitcast.14, s32[1]{0:T(128)S(6)} %copy.15.offset_ref, f32[1024,128]{1,0:T(8,128)S(1)} %bitcast.13, f32[2,256,128]{2,1,0:T(8,128)S(1)} %copy-done.1), custom_call_target="tpu_custom_call" | custom-call | flops 3000000000 | bytes 18874368 | tf_op jit(solution)/shard_map/beam/pallas_call | solution.py:397
  26.1 0.0 copy-done.5
  26.1 0.0 copy-done.2
  26.1 0.0 copy-done.4
  26.1 0.0 copy-done.6
  26.1 0.0 copy-done.7
  26.1 21.3 %fold.1 = (bf16[2,256,256]{2,1,0:T(8,128)(2,1)S(1)}, f32[5,128]{1,0:T(8,128)S(1)}) custom-call(bf16[2,2,2,256,256]{4,3,2,1,0:T(8,128)(2,1)S(1)} %get-tuple-element.8.data_ref, f32[2,2,256,256]{3,2,1,0:T(8,128)S(1)} %get-tuple-element.9.response_ref, s32[1,64]{1,0:T(1,128)S(1)} %copy-done.5, s32[512,128]{1,0:T(8,128)S(1)} %bitcast.15, ...), custom_call_target="tpu_custom_call" | custom-call | flops 6000000000 | bytes 6291456 | tf_op jit(solution)/shard_map/fold/pallas_call | solution.py:642
  47.4 0.8 %reshape.33 = bf16[2,1,65536]{2,0,1:T(2,128)(2,1)} reshape(bf16[2,256,256]{2,1,0:T(8,128)(2,1)S(1)} %get-tuple-element.10) | data formatting | bytes 524288 | tf_op jit(solution)/shard_map/reshape | solution.py:681
  48.2 0.5 %slice.9 = f32[1,64]{1,0:T(1,128)} slice(f32[5,128]{1,0:T(8,128)S(1)} %get-tuple-element.11), slice={[4:5], [0:64]} | slice | bytes 512 | tf_op jit(solution)/shard_map/slice | solution.py:682
  48.7 0.6 %slice_bitcast_fusion = (f32[256]{0:T(256)}, f32[2,128]{1,0:T(2,128)}) fusion(f32[5,128]{1,0:T(8,128)S(1)} %get-tuple-element.11), kind=kLoop, calls=%fused_computation | loop fusion | bytes 4096 | tf_op jit(solution)/shard_map/reshape | solution.py:684
Async XLA Ops:
  0.6 25.4 %copy-start.5 = (s32[1,64]{1,0:T(1,128)S(1)}, s32[1,64]{1,0:T(1,128)}, u32[]{:S(2)}) copy-start(s32[1,64]{1,0:T(1,128)} %flags_ref.1) | copy-start | bytes 772
  1.3 1.0 %copy-start = (f32[1,131072]{1,0:T(1,128)S(1)}, f32[1,131072]{1,0:T(1,128)}, u32[]{:S(2)}) copy-start(f32[1,131072]{1,0:T(1,128)} %param.12) | copy-start | bytes 1572868
  2.3 0.9 %copy-start.1 = (f32[2,256,128]{2,1,0:T(8,128)S(1)}, f32[2,256,128]{2,1,0:T(8,128)}, u32[]{:S(2)}) copy-start(f32[2,256,128]{2,1,0:T(8,128)} %constant.6.clone.turns_hbm.turns_ref) | copy-start | bytes 786436
  3.3 0.7 %copy-start.3 = (f32[2,64,1]{1,2,0:T(1,128)S(1)}, f32[2,64,1]{1,2,0:T(1,128)}, u32[]{:S(2)}) copy-start(f32[2,64,1]{1,2,0:T(1,128)} %param.11) | copy-start | bytes 1540
  4.0 22.1 %copy-start.2 = (f32[2,256,128]{2,1,0:T(8,128)S(1)}, f32[2,256,128]{2,1,0:T(8,128)}, u32[]{:S(2)}) copy-start(f32[2,256,128]{2,1,0:T(8,128)} %constant.6.clone.turns_hbm.turns_ref) | copy-start | bytes 786436
  4.0 22.1 %copy-start.4 = (s32[65536]{0:T(1024)S(1)}, s32[65536]{0:T(1024)}, u32[]{:S(2)}) copy-start(s32[65536]{0:T(1024)} %param.15) | copy-start | bytes 786436
  4.0 22.1 %copy-start.6 = (f32[2,2,256,256]{3,2,1,0:T(8,128)S(1)}, f32[2,2,256,256]{3,2,1,0:T(8,128)}, u32[]{:S(2)}) copy-start(f32[2,2,256,256]{3,2,1,0:T(8,128)} %constant.8.clone.twist_ref) | copy-start | bytes 3145732
  4.0 22.1 %copy-start.7 = (bf16[3,2,256,256]{3,2,1,0:T(8,128)(2,1)S(1)}, bf16[3,2,256,256]{3,2,1,0:T(8,128)(2,1)}, u32[]{:S(2)}) copy-start(bf16[3,2,256,256]{3,2,1,0:T(8,128)(2,1)} %constant.7.clone.dft_ref) | copy-start | bytes 2359300

commit v3 on v2

--- a/solution.py
+++ b/solution.py
@@ -27,7 +27,7 @@
 LOW_BINS = 32
 HIGH_BINS = BINS // LOW_BINS
 BLOCK_ROWS = 128
-STEP_LINES = 32
+STEP_LINES = 8
 LANES = 128
 DEPTH = 256
 PARTS = 4
@@ -49,7 +49,7 @@
 def dft_table():
     index = np.arange(COLS, dtype=np.int64)
     real, imag = unit_roots(index[:, None] * index[None, :], COLS)
-    return np.stack([bf16_split(real), bf16_split(imag), bf16_split(-imag)])
+    return bf16_split(np.concatenate([-imag, real, imag]))
 
 
 def twiddle():
@@ -160,9 +160,9 @@
 
 
 def beam_kernel(
-    antennas, pairs, volt_ref, gains_ref, offset_ref, chirp_hbm, turns_hbm, data_ref, response_ref,
+    antennas, pairs, volt_ref, gains_hbm, offset_ref, chirp_hbm, turns_hbm, data_ref, response_ref,
     table_ref, vbuf, pair_send, pair_recv, chip_send, chip_recv, own_ref, halo_send, halo_ref,
-    head_ref, chirp_ref, turns_ref, block_ref, load_sem, pair_sems, chip_sems, halo_sems,
+    head_ref, gains_ref, chirp_ref, turns_ref, block_ref, load_sem, pair_sems, chip_sems, halo_sems,
     head_sems, side_sems,
 ):
     count = 2 * pairs
@@ -193,6 +193,8 @@
             load(part, j, other).start()
         return carry
 
+    gains_copy = pltpu.make_async_copy(gains_hbm, gains_ref, side_sems.at[2])
+    gains_copy.start()
     lax.fori_loop(0, PARTS, begin, 0)
     side = [
         pltpu.make_async_copy(chirp_hbm, chirp_ref, side_sems.at[0]),
@@ -201,6 +203,7 @@
     for copy in side:
         copy.start()
     offset = offset_ref[0]
+    gains_copy.wait()
     weight_table(gains_ref, table_ref, antennas, me)
 
     def pair_copy(part, j):
@@ -393,14 +396,15 @@
     half = DEPTH // antennas // 2
     block = (2, PART_ROWS, COLS)
     vmem = pl.BlockSpec(memory_space=pltpu.VMEM)
-    hbm = pl.BlockSpec(memory_space=pl.ANY)
+    hbm = pl.BlockSpec(memory_space=pltpu.HBM)
+    keep = functools.partial(pltpu.with_memory_space_constraint, memory_space=pltpu.HBM)
     return pl.pallas_call(
         functools.partial(beam_kernel, antennas, pairs),
         out_shape=(
             jax.ShapeDtypeStruct((2, 2, 2, HALF_ROWS, COLS), jnp.bfloat16),
             jax.ShapeDtypeStruct((2, 2, HALF_ROWS, COLS), jnp.float32),
         ),
-        in_specs=[hbm, vmem, pl.BlockSpec(memory_space=pltpu.SMEM), hbm, hbm],
+        in_specs=[hbm, hbm, pl.BlockSpec(memory_space=pltpu.SMEM), hbm, hbm],
         out_specs=(vmem, vmem),
         scratch_shapes=[
             pltpu.VMEM((2, 8 * half, DEPTH), jnp.bfloat16),
@@ -413,6 +417,7 @@
             pltpu.VMEM((PARTS,) + block, jnp.bfloat16),
             pltpu.VMEM((PARTS,) + block, jnp.bfloat16),
             pltpu.VMEM((2, HALO_ROWS, COLS), jnp.bfloat16),
+            pltpu.VMEM(gains.shape, jnp.float32),
             pltpu.VMEM((NFFT // LANES, LANES), jnp.float32),
             pltpu.VMEM((2, HALF_ROWS, LANES), jnp.float32),
             pltpu.VMEM((LANES, LANES), jnp.float32),
@@ -421,7 +426,7 @@
             pltpu.SemaphoreType.DMA((2, PARTS, pairs - 1)),
             pltpu.SemaphoreType.DMA((2, PARTS)),
             pltpu.SemaphoreType.DMA((2,)),
-            pltpu.SemaphoreType.DMA((2,)),
+            pltpu.SemaphoreType.DMA((3,)),
         ],
         compiler_params=pltpu.CompilerParams(
             vmem_limit_bytes=44 << 20, collective_id=0, has_side_effects=True
@@ -430,12 +435,12 @@
             flops=3 * 10**9, bytes_accessed=18 << 20, transcendentals=0
         ),
         name="beam",
-    )(volts, gains, offset, chirp, jnp.asarray(half_turns()))
+    )(keep(volts), keep(gains), offset, keep(chirp), keep(jnp.asarray(half_turns())))
 
 
 def fold_kernel(
     chans, shards, data_ref, response_ref, flags_ref, bins_ref, dft_ref, twist_ref, turns_ref,
-    dedispersed_ref, small_ref, back_ref, weighted_ref, high_ref, low_ref, send_ref, recv_ref,
+    dedispersed_ref, small_ref, weighted_ref, high_ref, low_ref, send_ref, recv_ref,
     sems,
 ):
     everyone = chans * shards
@@ -452,35 +457,45 @@
         return carry
 
     lax.fori_loop(1, everyone, greet, 0)
-    def table(at):
-        return (dft_ref[at, 0], dft_ref[at, 1])
-
-    real_table, imag_table, minus_table = (table(0), table(1), table(2))
-
-    def ahead(tables, at):
-        return tuple(half[at] for half in tables)
-
+    def table(start, count=1):
+        rows = slice(start * COLS, (start + count) * COLS)
+        return (dft_ref[0, rows], dft_ref[1, rows])
+
+    minus_table, real_table, imag_table = (table(0), table(1), table(2))
+    forward, cross = (table(1, 2), table(0, 2))
+    pairs = []
     for kind in range(2):
         given = [(data_ref[kind, out, 0], data_ref[kind, out, 1]) for out in range(2)]
-        for start in range(0, HALF_ROWS, BLOCK_ROWS):
-            rows = slice(start, start + BLOCK_ROWS)
-            left, cross, minus = (
-                ahead(real_table, rows), ahead(imag_table, rows), ahead(minus_table, rows)
-            )
-            real = product((left, given[0]), (minus, given[1]))
-            imag = product((left, given[1]), (cross, given[0]))
-            cosine, sine = (twist_ref[0, kind, rows], twist_ref[1, kind, rows])
-            pair = (split(real * cosine - imag * sine), split(real * sine + imag * cosine))
-            real = product((pair[0], real_table), (pair[1], minus_table))
-            imag = product((pair[0], imag_table), (pair[1], real_table))
-            turn, tilt = (response_ref[0, kind, rows], response_ref[1, kind, rows])
-            pair = (split(real * turn - imag * tilt), split(real * tilt + imag * turn))
-            real = product((pair[0], real_table), (pair[1], imag_table))
-            imag = product((pair[0], minus_table), (pair[1], real_table))
-            for out, value in enumerate(
-                (real * cosine + imag * sine, imag * cosine - real * sine)
-            ):
-                back_ref[kind, out, 0, rows], back_ref[kind, out, 1, rows] = split(value)
+        both = product((forward, given[0]), (cross, given[1]))
+        pairs.append((both[:HALF_ROWS], both[HALF_ROWS:]))
+    for kind in range(2):
+        real, imag = pairs[kind]
+        cosine, sine = (twist_ref[0, kind], twist_ref[1, kind])
+        pairs[kind] = (split(real * cosine - imag * sine), split(real * sine + imag * cosine))
+    for kind in range(2):
+        real, imag = pairs[kind]
+        pairs[kind] = (
+            product((real, real_table), (imag, minus_table)),
+            product((real, imag_table), (imag, real_table)),
+        )
+    for kind in range(2):
+        real, imag = pairs[kind]
+        turn, tilt = (response_ref[0, kind], response_ref[1, kind])
+        pairs[kind] = (split(real * turn - imag * tilt), split(real * tilt + imag * turn))
+    for kind in range(2):
+        real, imag = pairs[kind]
+        pairs[kind] = (
+            product((real, real_table), (imag, imag_table)),
+            product((real, minus_table), (imag, real_table)),
+        )
+    for kind in range(2):
+        real, imag = pairs[kind]
+        cosine, sine = (twist_ref[0, kind], twist_ref[1, kind])
+        pairs[kind] = (split(real * cosine + imag * sine), split(imag * cosine - real * sine))
+    for kind in range(2):
+        real, imag = pairs[kind]
+        both = product((cross, real), (forward, imag))
+        pairs[kind] = (both[HALF_ROWS:], both[:HALF_ROWS])
 
     flag = flags_ref[...]
     if WINDOWS < LANES:
@@ -503,22 +518,10 @@
     weight_row = jnp.zeros((1, LANES), jnp.float32)
     for start in range(0, HALF_ROWS, BLOCK_ROWS):
         rows = slice(start, start + BLOCK_ROWS)
-        left, cross, minus = (
-            ahead(real_table, rows), ahead(imag_table, rows), ahead(minus_table, rows)
-        )
-        parts = []
-        for kind in range(2):
-            given = [(back_ref[kind, out, 0], back_ref[kind, out, 1]) for out in range(2)]
-            parts.append(
-                (
-                    product((left, given[0]), (cross, given[1])),
-                    product((left, given[1]), (minus, given[0])),
-                )
-            )
         cosine, sine = [
             jnp.concatenate([turns_ref[out, rows]] * (COLS // LANES), axis=1) for out in range(2)
         ]
-        (real, imag), (odd_real, odd_imag) = parts
+        (real, imag), (odd_real, odd_imag) = [[value[rows] for value in pair] for pair in pairs]
         real = real - (odd_real * cosine + odd_imag * sine)
         imag = imag - (odd_imag * cosine - odd_real * sine)
         dedispersed_ref[0, rows] = real.astype(jnp.bfloat16)
@@ -552,7 +555,7 @@
     high_index = high_index.astype(jnp.float32).astype(jnp.bfloat16)
     low_index = lax.broadcasted_iota(jnp.int32, (LOW_BINS, LANES), 0)
     low_index = low_index.astype(jnp.float32).astype(jnp.bfloat16)
-    one, zero = (jnp.bfloat16(1.0), jnp.bfloat16(0.0))
+    minus, zero = (jnp.bfloat16(-1.0), jnp.bfloat16(0.0))
 
     def step(at, total):
         start = at * STEP_LINES
@@ -564,19 +567,20 @@
         lines_here = pl.ds(start, STEP_LINES)
         highs, lows, values = (high_ref[lines_here], low_ref[lines_here], weighted_ref[lines_here])
         for line in range(STEP_LINES):
-            left.append(jnp.where(high_index == spread(highs, line, HIGH_BINS), one, zero))
+            left.append(jnp.where(high_index == spread(highs, line, HIGH_BINS), minus, zero))
             value = spread(values, line, LOW_BINS)
             right.append(jnp.where(low_index == spread(lows, line, LOW_BINS), value, zero))
-        return total + lax.dot_general(
+        return total - lax.dot_general(
             jnp.concatenate(left, axis=1),
             jnp.concatenate(right, axis=1),
             ((((1,), (1,))), ((), ())),
             preferred_element_type=jnp.float32,
         )
 
-    total = jnp.zeros((HIGH_BINS, LOW_BINS), jnp.float32)
+    totals = [jnp.zeros((HIGH_BINS, LOW_BINS), jnp.float32)] * 2
     for at in range(HALF_ROWS * per_line // STEP_LINES):
-        total = step(at, total)
+        totals[at % 2] = step(at, totals[at % 2])
+    total = totals[0] + totals[1]
     per_row = LANES // LOW_BINS
     total = jnp.concatenate([total, jnp.zeros((HIGH_BINS, LANES - LOW_BINS), jnp.float32)], axis=1)
     place = lax.broadcasted_iota(jnp.int32, (HIGH_BINS, LANES), 0) % per_row
@@ -648,7 +652,6 @@
         in_specs=[vmem] * 7,
         out_specs=(vmem,) * 2,
         scratch_shapes=[
-            pltpu.VMEM((2, 2, 2, HALF_ROWS, COLS), jnp.bfloat16),
             pltpu.VMEM((HALF_ROWS * COLS // LANES, LANES), jnp.float32),
             pltpu.VMEM((HALF_ROWS * COLS // LANES, LANES), jnp.float32),
             pltpu.VMEM((HALF_ROWS * COLS // LANES, LANES), jnp.float32),

time: 49.5 us -> 44.1 us (0.89)
  Pallas kernels: 43.4 us -> 40.6 us
  local copies, waits for them, and re-layouts: 4.54 us -> 1.88 us
    pallas_call x1, Pallas kernels: 21.3 us -> 16.2 us  [fold(): pl.pallas_call(functools.partial(fold_kernel, chans, shards), out_shape=(...]
    unnamed x16 -> x10, local copies, waits for them, and re-layouts: 2.68 us -> 0.03 us
    pallas_call x1, Pallas kernels: 22.1 us -> 24.4 us  [beam(): pl.pallas_call(functools.partial(beam_kernel, antennas, pairs), out_shape...]
where the time goes in v3:
time: 44.1 us; the launch traced here: 44 us
  Pallas kernels  40.6 us (92%)
  local copies, waits for them, and re-layouts  1.88 us (4%)
  between operations  1.52 us (3%)
    pallas_call x1, Pallas kernels, beam(): pl.pallas_call(functools.partial(beam_kernel, antennas, pairs), out_shape...  24.4 us
    pallas_call x1, Pallas kernels, fold(): pl.pallas_call(functools.partial(fold_kernel, chans, shards), out_shape=(...  16.2 us

profile of v3, /device:TPU:0, one launch (start us, length us, event | category | flops | bytes accessed | tf_op | source)
XLA Modules:
  0.0 44.0 jit_solution(2715108609804998009)
XLA Ops:
  0.6 0.0 copy-start
  0.6 0.0 copy-start.3
  0.7 0.0 copy-start.4
  0.7 0.0 copy-start.1
  0.7 0.0 copy-start.2
  1.5 24.4 %beam.1 = (bf16[2,2,2,256,256]{4,3,2,1,0:T(8,128)(2,1)S(1)}, f32[2,2,256,256]{3,2,1,0:T(8,128)S(1)}) custom-call(bf16[2,32768,128]{2,1,0:T(8,128)(2,1)} %bitcast.14, f32[2,1,64]{2,1,0:T(1,128)} %bitcast.17, s32[1]{0:T(128)S(6)} %copy.15.offset_ref, f32[1024,128]{1,0:T(8,128)} %bitcast.15, f32[2,256,128]{2,1,0:T(8,128)} %constant.6.clone.turns_hbm.turns_ref), custom_call_target="tpu_custom_call" | custom-call | flops 3000000000 | bytes 18874368 | tf_op jit(solution)/shard_map/beam/pallas_call | solution.py:401
  25.8 0.0 copy-done
  25.9 0.0 copy-done.3
  25.9 0.0 copy-done.4
  25.9 0.0 copy-done.1
  25.9 0.0 copy-done.2
  25.9 16.2 %fold.1 = (bf16[2,256,256]{2,1,0:T(8,128)(2,1)S(1)}, f32[5,128]{1,0:T(8,128)S(1)}) custom-call(bf16[2,2,2,256,256]{4,3,2,1,0:T(8,128)(2,1)S(1)} %get-tuple-element.8.data_ref, f32[2,2,256,256]{3,2,1,0:T(8,128)S(1)} %get-tuple-element.9.response_ref, s32[1,64]{1,0:T(1,128)S(1)} %copy-done.2, s32[512,128]{1,0:T(8,128)S(1)} %bitcast.13, ...), custom_call_target="tpu_custom_call" | custom-call | flops 6000000000 | bytes 6291456 | tf_op jit(solution)/shard_map/fold/pallas_call | solution.py:646
  42.1 0.8 %reshape.33 = bf16[2,1,65536]{2,0,1:T(2,128)(2,1)} reshape(bf16[2,256,256]{2,1,0:T(8,128)(2,1)S(1)} %get-tuple-element.10) | data formatting | bytes 524288 | tf_op jit(solution)/shard_map/reshape | solution.py:684
  42.9 0.5 %slice.9 = f32[1,64]{1,0:T(1,128)} slice(f32[5,128]{1,0:T(8,128)S(1)} %get-tuple-element.11), slice={[4:5], [0:64]} | slice | bytes 512 | tf_op jit(solution)/shard_map/slice | solution.py:685
  43.4 0.6 %slice_bitcast_fusion = (f32[256]{0:T(256)}, f32[2,128]{1,0:T(2,128)}) fusion(f32[5,128]{1,0:T(8,128)S(1)} %get-tuple-element.11), kind=kLoop, calls=%fused_computation | loop fusion | bytes 4096 | tf_op jit(solution)/shard_map/reshape | solution.py:687
Async XLA Ops:
  0.6 25.2 %copy-start = (f32[2,256,128]{2,1,0:T(8,128)S(1)}, f32[2,256,128]{2,1,0:T(8,128)}, u32[]{:S(2)}) copy-start(f32[2,256,128]{2,1,0:T(8,128)} %constant.6.clone.turns_hbm.turns_ref) | copy-start | bytes 786436
  0.6 25.2 %copy-start.3 = (f32[2,2,256,256]{3,2,1,0:T(8,128)S(1)}, f32[2,2,256,256]{3,2,1,0:T(8,128)}, u32[]{:S(2)}) copy-start(f32[2,2,256,256]{3,2,1,0:T(8,128)} %constant.8.clone.twist_ref) | copy-start | bytes 3145732
  0.7 25.2 %copy-start.4 = (bf16[2,768,256]{2,1,0:T(8,128)(2,1)S(1)}, bf16[2,768,256]{2,1,0:T(8,128)(2,1)}, u32[]{:S(2)}) copy-start(bf16[2,768,256]{2,1,0:T(8,128)(2,1)} %constant.7.clone.dft_ref) | copy-start | bytes 2359300
  0.7 25.2 %copy-start.1 = (s32[65536]{0:T(1024)S(1)}, s32[65536]{0:T(1024)}, u32[]{:S(2)}) copy-start(s32[65536]{0:T(1024)} %param.15) | copy-start | bytes 786436
  0.7 25.2 %copy-start.2 = (s32[1,64]{1,0:T(1,128)S(1)}, s32[1,64]{1,0:T(1,128)}, u32[]{:S(2)}) copy-start(s32[1,64]{1,0:T(1,128)} %flags_ref.1) | copy-start | bytes 772

commit v4 on v3

--- a/solution.py
+++ b/solution.py
@@ -30,7 +30,7 @@
 STEP_LINES = 8
 LANES = 128
 DEPTH = 256
-PARTS = 4
+PARTS = 8
 PART_ROWS = HALF_ROWS // PARTS
 MESH = pl.DeviceIdType.MESH
 
@@ -175,22 +175,35 @@
         )
     size = vbuf.shape[3]
 
-    def shard_of(j, other):
-        return lax.rem(pair + 1 + j, pairs) * 2 + (1 - core if other else core)
-
-    def load(part, j, other):
-        start = pl.multiple_of((shard_of(j, other) * PARTS + part) * size, size)
-        slot = 2 * j + (0 if other else 1)
+    levels = pairs.bit_length() - 1
+    roles = sorted(range(pairs), key=lambda role: (role & 1 == 0, -role))
+
+    def bit(level, side):
+        return jnp.where(side == 0, 1 << level, 1 << (level + 1) % levels)
+
+    def across(level, side):
+        amount = bit(level, side)
+        return amount * (1 - 2 * lax.rem(pair // amount, 2))
+
+    def shard_of(role, other):
+        side = 1 - core if other else core
+        place = pair
+        for level in range(levels):
+            if role >> level & 1:
+                place = place + across(level, side)
+        return place * 2 + side
+
+    def load(part, role, other):
+        start = pl.multiple_of((shard_of(role, other) * PARTS + part) * size, size)
+        slot = 2 * role + (0 if other else 1)
         return pltpu.make_async_copy(
             volt_ref.at[:, pl.ds(start, size)], vbuf.at[part, slot], load_sem.at[part, slot]
         )
 
-    def order():
-        return [(j, True) for j in range(pairs)] + [(j, False) for j in range(pairs)]
-
     def begin(part, carry):
-        for j, other in order():
-            load(part, j, other).start()
+        for other in (True, False):
+            for role in roles:
+                load(part, role, other).start()
         return carry
 
     gains_copy = pltpu.make_async_copy(gains_hbm, gains_ref, side_sems.at[2])
@@ -206,18 +219,23 @@
     gains_copy.wait()
     weight_table(gains_ref, table_ref, antennas, me)
 
-    def pair_copy(part, j):
+    def pair_copy(part, role):
         return pltpu.make_async_remote_copy(
-            src_ref=pair_send.at[part, j], dst_ref=pair_recv.at[part, j],
-            send_sem=pair_sems.at[0, part, j], recv_sem=pair_sems.at[1, part, j],
+            src_ref=pair_send.at[part, role], dst_ref=pair_recv.at[part, role],
+            send_sem=pair_sems.at[0, part, role], recv_sem=pair_sems.at[1, part, role],
             device_id={"tm": pair * 2 + (1 - core)}, device_id_type=MESH,
         )
 
-    def chip_copy(part, j):
+    def level_of(role):
+        return (role & -role).bit_length() - 1
+
+    def chip_copy(part, role):
+        slot = role - 1
         return pltpu.make_async_remote_copy(
-            src_ref=chip_send.at[part, j], dst_ref=chip_recv.at[part, j],
-            send_sem=chip_sems.at[0, part, j], recv_sem=chip_sems.at[1, part, j],
-            device_id={"tm": shard_of(j, False)}, device_id_type=MESH,
+            src_ref=chip_send.at[part, slot], dst_ref=chip_recv.at[part, slot],
+            send_sem=chip_sems.at[0, part, slot], recv_sem=chip_sems.at[1, part, slot],
+            device_id={"tm": (pair + across(level_of(role), core)) * 2 + core},
+            device_id_type=MESH,
         )
 
     def halo_copy(part):
@@ -234,14 +252,22 @@
             device_id={"tm": lax.rem(me + count - 1, count)}, device_id_type=MESH,
         )
 
+    def pass_on(part, level):
+        for role in roles:
+            if role & ((2 << level) - 1) == 0:
+                source = role + (1 << level)
+                chip_copy(part, source).wait_recv()
+                total = own_ref[part, role // 2] + chip_recv[part, source - 1].astype(jnp.float32)
+                if role and level_of(role) == level + 1:
+                    chip_send[part, role - 1] = total.astype(jnp.bfloat16)
+                    chip_copy(part, role).start()
+                else:
+                    own_ref[part, role // 2] = total
+                    if role == 0 and level == levels - 1:
+                        halo_send[part] = total.astype(jnp.bfloat16)
+
     def finish(part):
-        for j in range(pairs - 1):
-            chip_copy(part, j).wait_recv()
-        total = own_ref[part]
-        for j in range(pairs - 1):
-            total = total + chip_recv[part, j].astype(jnp.float32)
-        own_ref[part] = total
-        halo_send[part] = total.astype(jnp.bfloat16)
+        pass_on(part, levels - 1)
 
         @pl.when(me < count - 1)
         def _():
@@ -270,7 +296,7 @@
                 jnp.concatenate([head, value[HALO_ROWS:]], axis=0)
                 for head, value in zip(first, before)
             ]
-        after = [own_ref[part, 0], own_ref[part, 1]]
+        after = [own_ref[part, 0, 0], own_ref[part, 0, 1]]
         real, imag = (before[0] - after[0], before[1] - after[1])
         cosine, sine = [
             jnp.concatenate([turns_ref[out, rows]] * (COLS // LANES), axis=1) for out in range(2)
@@ -284,45 +310,47 @@
                 data_ref[kind, out, 0, rows], data_ref[kind, out, 1, rows] = split(value)
 
     def run(part, carry):
-        for j in range(pairs):
-            load(part, j, True).wait()
-
-            def put(out, at, rows, value, j=j):
-                pair_send[part, j, out, at : at + rows] = value
-
-            part_beam(table_ref, vbuf.at[part, 2 * j], antennas, put)
-            if j == 0:
+        for role in roles:
+            load(part, role, True).wait()
+
+            def put(out, at, rows, value, role=role):
+                pair_send[part, role, out, at : at + rows] = value
+
+            part_beam(table_ref, vbuf.at[part, 2 * role], antennas, put)
+            if role == roles[0]:
 
                 @pl.when(part == 0)
                 def _():
                     pl.semaphore_wait(barrier, count - 1)
 
-            pair_copy(part, j).start()
-        for j in range(pairs):
-            load(part, j, False).wait()
-            pair_copy(part, j).wait_recv()
-            if j < pairs - 1:
-
-                def put(out, at, rows, value, j=j):
-                    value = value + pair_recv[part, j, out, at : at + rows]
-                    chip_send[part, j, out, at : at + rows] = value.astype(jnp.bfloat16)
-
-            else:
-
-                def put(out, at, rows, value, j=j):
-                    value = value + pair_recv[part, j, out, at : at + rows]
-                    own_ref[part, out, at : at + rows] = value
-
-            part_beam(table_ref, vbuf.at[part, 2 * j + 1], antennas, put)
-            if j < pairs - 1:
-                chip_copy(part, j).start()
-
-        @pl.when(part == 0)
+            pair_copy(part, role).start()
+        for role in roles:
+            load(part, role, False).wait()
+            pair_copy(part, role).wait_recv()
+
+            def put(out, at, rows, value, role=role):
+                value = value + pair_recv[part, role, out, at : at + rows]
+                if role % 2:
+                    chip_send[part, role - 1, out, at : at + rows] = value.astype(jnp.bfloat16)
+                else:
+                    own_ref[part, role // 2, out, at : at + rows] = value
+
+            part_beam(table_ref, vbuf.at[part, 2 * role + 1], antennas, put)
+            if role % 2:
+                chip_copy(part, role).start()
+        return carry
+
+    lax.fori_loop(0, PARTS, run, 0)
+    for copy in side:
+        copy.wait()
+
+    def settle(part, carry):
+        for level in range(levels - 1):
+            pass_on(part, level)
+
+        @pl.when(part < ROWS // LANES)
         def _():
-            for copy in side:
-                copy.wait()
-
-        chirp_block(part)
+            chirp_block(part)
 
         @pl.when(part > 0)
         def _():
@@ -334,7 +362,7 @@
 
         return carry
 
-    lax.fori_loop(0, PARTS, run, 0)
+    lax.fori_loop(0, PARTS, settle, 0)
     finish(PARTS - 1)
 
     @pl.when(me == 0)
@@ -380,10 +408,10 @@
             halo_copy(part).wait_send()
 
     def drain(part, carry):
-        for j in range(pairs):
-            pair_copy(part, j).wait_send()
-            if j < pairs - 1:
-                chip_copy(part, j).wait_send()
+        for role in roles:
+            pair_copy(part, role).wait_send()
+            if role:
+                chip_copy(part, role).wait_send()
         return carry
 
     lax.fori_loop(0, PARTS, drain, 0)
@@ -413,7 +441,7 @@
             pltpu.VMEM((PARTS, pairs) + block, jnp.float32),
             pltpu.VMEM((PARTS, pairs - 1) + block, jnp.bfloat16),
             pltpu.VMEM((PARTS, pairs - 1) + block, jnp.bfloat16),
-            pltpu.VMEM((PARTS,) + block, jnp.float32),
+            pltpu.VMEM((PARTS, pairs // 2) + block, jnp.float32),
             pltpu.VMEM((PARTS,) + block, jnp.bfloat16),
             pltpu.VMEM((PARTS,) + block, jnp.bfloat16),
             pltpu.VMEM((2, HALO_ROWS, COLS), jnp.bfloat16),
@@ -672,7 +700,7 @@
 def on_device(voltages, antenna_gains, chirp_phase, offsets, flags, sample_phase_bins):
     shards, chans = (lax.axis_size("tm"), lax.axis_size("chan"))
     antennas, channels, samples = voltages.shape[1:]
-    assert channels == 1 and shards % 2 == 0
+    assert channels == 1 and shards >= 4 and shards & (shards - 1) == 0
     volts = voltages.reshape(2, antennas, samples // LANES, LANES)
     volts = jnp.transpose(volts, (0, 2, 1, 3)).reshape(2, samples // LANES * antennas, LANES)
     gains = jnp.transpose(antenna_gains, (0, 2, 1))

time: 44.1 us -> 53.8 us (1.22)
  Pallas kernels: 40.6 us -> 50.2 us
    pallas_call x1, Pallas kernels: 24.4 us -> 35.3 us  [beam(): pl.pallas_call(functools.partial(beam_kernel, antennas, pairs), out_shape...]
    pallas_call x1, Pallas kernels: 16.2 us -> 14.8 us  [fold(): pl.pallas_call(functools.partial(fold_kernel, chans, shards), out_shape=(...]
where the time goes in v4:
time: 53.8 us; the launch traced here: 53.6 us
  Pallas kernels  50.2 us (93%)
  local copies, waits for them, and re-layouts  1.88 us (3%)
  between operations  1.52 us (3%)
    pallas_call x1, Pallas kernels, beam(): pl.pallas_call(functools.partial(beam_kernel, antennas, pairs), out_shape...  35.3 us
    pallas_call x1, Pallas kernels, fold(): pl.pallas_call(functools.partial(fold_kernel, chans, shards), out_shape=(...  14.8 us

profile of v4, /device:TPU:0, one launch (start us, length us, event | category | flops | bytes accessed | tf_op | source)
XLA Modules:
  0.0 53.6 jit_solution(4883069458632538046)
XLA Ops:
  0.6 0.0 copy-start
  0.6 0.0 copy-start.3
  0.7 0.0 copy-start.4
  0.7 0.0 copy-start.1
  0.7 0.0 copy-start.2
  1.5 35.3 %beam.1 = (bf16[2,2,2,256,256]{4,3,2,1,0:T(8,128)(2,1)S(1)}, f32[2,2,256,256]{3,2,1,0:T(8,128)S(1)}) custom-call(bf16[2,32768,128]{2,1,0:T(8,128)(2,1)} %bitcast.14, f32[2,1,64]{2,1,0:T(1,128)} %bitcast.17, s32[1]{0:T(128)S(6)} %copy.15.offset_ref, f32[1024,128]{1,0:T(8,128)} %bitcast.15, f32[2,256,128]{2,1,0:T(8,128)} %constant.6.clone.turns_hbm.turns_ref), custom_call_target="tpu_custom_call" | custom-call | flops 3000000000 | bytes 18874368 | tf_op jit(solution)/shard_map/beam/pallas_call | solution.py:429
  36.8 0.0 copy-done
  36.8 0.0 copy-done.3
  36.8 0.0 copy-done.4
  36.9 0.0 copy-done.1
  36.9 0.0 copy-done.2
  36.9 14.8 %fold.1 = (bf16[2,256,256]{2,1,0:T(8,128)(2,1)S(1)}, f32[5,128]{1,0:T(8,128)S(1)}) custom-call(bf16[2,2,2,256,256]{4,3,2,1,0:T(8,128)(2,1)S(1)} %get-tuple-element.8.data_ref, f32[2,2,256,256]{3,2,1,0:T(8,128)S(1)} %get-tuple-element.9.response_ref, s32[1,64]{1,0:T(1,128)S(1)} %copy-done.2, s32[512,128]{1,0:T(8,128)S(1)} %bitcast.13, ...), custom_call_target="tpu_custom_call" | custom-call | flops 6000000000 | bytes 6291456 | tf_op jit(solution)/shard_map/fold/pallas_call | solution.py:674
  51.7 0.8 %reshape.33 = bf16[2,1,65536]{2,0,1:T(2,128)(2,1)} reshape(bf16[2,256,256]{2,1,0:T(8,128)(2,1)S(1)} %get-tuple-element.10) | data formatting | bytes 524288 | tf_op jit(solution)/shard_map/reshape | solution.py:712
  52.5 0.5 slice.9
  53.0 0.6 %slice_bitcast_fusion = (f32[256]{0:T(256)}, f32[2,128]{1,0:T(2,128)}) fusion(f32[5,128]{1,0:T(8,128)S(1)} %get-tuple-element.11), kind=kLoop, calls=%fused_computation | loop fusion | bytes 4096 | tf_op jit(solution)/shard_map/reshape | solution.py:715
Async XLA Ops:
  0.6 36.2 %copy-start = (f32[2,256,128]{2,1,0:T(8,128)S(1)}, f32[2,256,128]{2,1,0:T(8,128)}, u32[]{:S(2)}) copy-start(f32[2,256,128]{2,1,0:T(8,128)} %constant.6.clone.turns_hbm.turns_ref) | copy-start | bytes 786436
  0.6 36.2 %copy-start.3 = (f32[2,2,256,256]{3,2,1,0:T(8,128)S(1)}, f32[2,2,256,256]{3,2,1,0:T(8,128)}, u32[]{:S(2)}) copy-start(f32[2,2,256,256]{3,2,1,0:T(8,128)} %constant.8.clone.twist_ref) | copy-start | bytes 3145732
  0.7 36.2 %copy-start.4 = (bf16[2,768,256]{2,1,0:T(8,128)(2,1)S(1)}, bf16[2,768,256]{2,1,0:T(8,128)(2,1)}, u32[]{:S(2)}) copy-start(bf16[2,768,256]{2,1,0:T(8,128)(2,1)} %constant.7.clone.dft_ref) | copy-start | bytes 2359300
  0.7 36.2 %copy-start.1 = (s32[65536]{0:T(1024)S(1)}, s32[65536]{0:T(1024)}, u32[]{:S(2)}) copy-start(s32[65536]{0:T(1024)} %param.15) | copy-start | bytes 786436
  0.7 36.2 %copy-start.2 = (s32[1,64]{1,0:T(1,128)S(1)}, s32[1,64]{1,0:T(1,128)}, u32[]{:S(2)}) copy-start(s32[1,64]{1,0:T(1,128)} %flags_ref.1) | copy-start | bytes 772

commit v5 on v4

--- a/solution.py
+++ b/solution.py
@@ -31,6 +31,8 @@
 LANES = 128
 DEPTH = 256
 PARTS = 8
+PAIR_LAG = 2
+CHIP_LAG = 5
 PART_ROWS = HALF_ROWS // PARTS
 MESH = pl.DeviceIdType.MESH
 
@@ -200,15 +202,22 @@
             volt_ref.at[:, pl.ds(start, size)], vbuf.at[part, slot], load_sem.at[part, slot]
         )
 
-    def begin(part, carry):
-        for other in (True, False):
+    def begin(step, carry):
+        @pl.when(step < PARTS)
+        def _():
             for role in roles:
-                load(part, role, other).start()
+                load(step, role, True).start()
+
+        @pl.when(step >= PAIR_LAG)
+        def _():
+            for role in roles:
+                load(step - PAIR_LAG, role, False).start()
+
         return carry
 
     gains_copy = pltpu.make_async_copy(gains_hbm, gains_ref, side_sems.at[2])
     gains_copy.start()
-    lax.fori_loop(0, PARTS, begin, 0)
+    lax.fori_loop(0, PARTS + PAIR_LAG, begin, 0)
     side = [
         pltpu.make_async_copy(chirp_hbm, chirp_ref, side_sems.at[0]),
         pltpu.make_async_copy(turns_hbm, turns_ref, side_sems.at[1]),
@@ -219,23 +228,29 @@
     gains_copy.wait()
     weight_table(gains_ref, table_ref, antennas, me)
 
-    def pair_copy(part, role):
+    def pair_copy(part):
         return pltpu.make_async_remote_copy(
-            src_ref=pair_send.at[part, role], dst_ref=pair_recv.at[part, role],
-            send_sem=pair_sems.at[0, part, role], recv_sem=pair_sems.at[1, part, role],
+            src_ref=pair_send.at[part], dst_ref=pair_recv.at[part],
+            send_sem=pair_sems.at[0, part], recv_sem=pair_sems.at[1, part],
             device_id={"tm": pair * 2 + (1 - core)}, device_id_type=MESH,
         )
 
     def level_of(role):
         return (role & -role).bit_length() - 1
 
-    def chip_copy(part, role):
-        slot = role - 1
+    def first_slot(level):
+        return pairs - (pairs >> level)
+
+    def slot_of(role):
+        level = level_of(role)
+        return first_slot(level) + (role >> (level + 1))
+
+    def chip_copy(part, level):
+        slots = slice(first_slot(level), first_slot(level + 1))
         return pltpu.make_async_remote_copy(
-            src_ref=chip_send.at[part, slot], dst_ref=chip_recv.at[part, slot],
-            send_sem=chip_sems.at[0, part, slot], recv_sem=chip_sems.at[1, part, slot],
-            device_id={"tm": (pair + across(level_of(role), core)) * 2 + core},
-            device_id_type=MESH,
+            src_ref=chip_send.at[part, slots], dst_ref=chip_recv.at[part, slots],
+            send_sem=chip_sems.at[0, part, level], recv_sem=chip_sems.at[1, part, level],
+            device_id={"tm": (pair + across(level, core)) * 2 + core}, device_id_type=MESH,
         )
 
     def halo_copy(part):
@@ -253,18 +268,19 @@
         )
 
     def pass_on(part, level):
+        chip_copy(part, level).wait_recv()
         for role in roles:
             if role & ((2 << level) - 1) == 0:
-                source = role + (1 << level)
-                chip_copy(part, source).wait_recv()
-                total = own_ref[part, role // 2] + chip_recv[part, source - 1].astype(jnp.float32)
+                arrived = chip_recv[part, slot_of(role + (1 << level))].astype(jnp.float32)
+                total = own_ref[part, role // 2] + arrived
                 if role and level_of(role) == level + 1:
-                    chip_send[part, role - 1] = total.astype(jnp.bfloat16)
-                    chip_copy(part, role).start()
+                    chip_send[part, slot_of(role)] = total.astype(jnp.bfloat16)
                 else:
                     own_ref[part, role // 2] = total
                     if role == 0 and level == levels - 1:
                         halo_send[part] = total.astype(jnp.bfloat16)
+        if level < levels - 1:
+            chip_copy(part, level + 1).start()
 
     def finish(part):
         pass_on(part, levels - 1)
@@ -309,61 +325,74 @@
             for out, value in enumerate(values):
                 data_ref[kind, out, 0, rows], data_ref[kind, out, 1, rows] = split(value)
 
-    def run(part, carry):
+    def give(part):
         for role in roles:
             load(part, role, True).wait()
+        for role in roles:
 
             def put(out, at, rows, value, role=role):
                 pair_send[part, role, out, at : at + rows] = value
 
             part_beam(table_ref, vbuf.at[part, 2 * role], antennas, put)
-            if role == roles[0]:
-
-                @pl.when(part == 0)
-                def _():
-                    pl.semaphore_wait(barrier, count - 1)
-
-            pair_copy(part, role).start()
+
+        @pl.when(part == 0)
+        def _():
+            pl.semaphore_wait(barrier, count - 1)
+
+        pair_copy(part).start()
+
+    def take(part):
         for role in roles:
             load(part, role, False).wait()
-            pair_copy(part, role).wait_recv()
+        pair_copy(part).wait_recv()
+        for role in roles:
 
             def put(out, at, rows, value, role=role):
                 value = value + pair_recv[part, role, out, at : at + rows]
                 if role % 2:
-                    chip_send[part, role - 1, out, at : at + rows] = value.astype(jnp.bfloat16)
+                    chip_send[part, slot_of(role), out, at : at + rows] = value.astype(jnp.bfloat16)
                 else:
                     own_ref[part, role // 2, out, at : at + rows] = value
 
             part_beam(table_ref, vbuf.at[part, 2 * role + 1], antennas, put)
-            if role % 2:
-                chip_copy(part, role).start()
+        chip_copy(part, 0).start()
+
+    def run(step, carry):
+        @pl.when(step < PARTS)
+        def _():
+            give(step)
+
+        @pl.when(step >= PAIR_LAG)
+        def _():
+            take(step - PAIR_LAG)
+
         return carry
 
-    lax.fori_loop(0, PARTS, run, 0)
+    lax.fori_loop(0, PARTS + PAIR_LAG, run, 0)
     for copy in side:
         copy.wait()
 
-    def settle(part, carry):
-        for level in range(levels - 1):
-            pass_on(part, level)
-
-        @pl.when(part < ROWS // LANES)
-        def _():
-            chirp_block(part)
-
-        @pl.when(part > 0)
-        def _():
-            finish(part - 1)
-
-            @pl.when((part == 1) & (me > 0))
+    def settle(step, carry):
+        @pl.when(step < PARTS)
+        def _():
+            for level in range(levels - 1):
+                pass_on(step, level)
+
+        @pl.when(step < ROWS // LANES)
+        def _():
+            chirp_block(step)
+
+        @pl.when(step >= CHIP_LAG)
+        def _():
+            finish(step - CHIP_LAG)
+
+            @pl.when((step == CHIP_LAG) & (me > 0))
             def _():
                 head_copy().start()
 
         return carry
 
-    lax.fori_loop(0, PARTS, settle, 0)
-    finish(PARTS - 1)
+    lax.fori_loop(0, PARTS + CHIP_LAG, settle, 0)
 
     @pl.when(me == 0)
     def _():
@@ -408,10 +437,9 @@
             halo_copy(part).wait_send()
 
     def drain(part, carry):
-        for role in roles:
-            pair_copy(part, role).wait_send()
-            if role:
-                chip_copy(part, role).wait_send()
+        pair_copy(part).wait_send()
+        for level in range(levels):
+            chip_copy(part, level).wait_send()
         return carry
 
     lax.fori_loop(0, PARTS, drain, 0)
@@ -450,8 +478,8 @@
             pltpu.VMEM((2, HALF_ROWS, LANES), jnp.float32),
             pltpu.VMEM((LANES, LANES), jnp.float32),
             pltpu.SemaphoreType.DMA((PARTS, shards)),
-            pltpu.SemaphoreType.DMA((2, PARTS, pairs)),
-            pltpu.SemaphoreType.DMA((2, PARTS, pairs - 1)),
+            pltpu.SemaphoreType.DMA((2, PARTS)),
+            pltpu.SemaphoreType.DMA((2, PARTS, pairs.bit_length() - 1)),
             pltpu.SemaphoreType.DMA((2, PARTS)),
             pltpu.SemaphoreType.DMA((2,)),
             pltpu.SemaphoreType.DMA((3,)),

time: 53.8 us -> 38.7 us (0.72)
  Pallas kernels: 50.2 us -> 35.1 us
    pallas_call x1, Pallas kernels: 35.3 us -> 20 us  [beam(): pl.pallas_call(functools.partial(beam_kernel, antennas, pairs), out_shape...]
where the time goes in v5:
time: 38.7 us; the launch traced here: 38.5 us
  Pallas kernels  35.1 us (91%)
  local copies, waits for them, and re-layouts  1.88 us (5%)
  between operations  1.52 us (4%)
    pallas_call x1, Pallas kernels, beam(): pl.pallas_call(functools.partial(beam_kernel, antennas, pairs), out_shape...  20 us
    pallas_call x1, Pallas kernels, fold(): pl.pallas_call(functools.partial(fold_kernel, chans, shards), out_shape=(...  15.1 us

profile of v5, /device:TPU:0, one launch (start us, length us, event | category | flops | bytes accessed | tf_op | source)
XLA Modules:
  0.0 38.5 jit_solution(12013445388217512223)
XLA Ops:
  0.6 0.0 copy-start
  0.6 0.0 copy-start.3
  0.7 0.0 copy-start.4
  0.7 0.0 copy-start.1
  0.7 0.0 copy-start.2
  1.5 20.0 %beam.1 = (bf16[2,2,2,256,256]{4,3,2,1,0:T(8,128)(2,1)S(1)}, f32[2,2,256,256]{3,2,1,0:T(8,128)S(1)}) custom-call(bf16[2,32768,128]{2,1,0:T(8,128)(2,1)} %bitcast.14, f32[2,1,64]{2,1,0:T(1,128)} %bitcast.17, s32[1]{0:T(128)S(6)} %copy.15.offset_ref, f32[1024,128]{1,0:T(8,128)} %bitcast.15, f32[2,256,128]{2,1,0:T(8,128)} %constant.6.clone.turns_hbm.turns_ref), custom_call_target="tpu_custom_call" | custom-call | flops 3000000000 | bytes 18874368 | tf_op jit(solution)/shard_map/beam/pallas_call | solution.py:457
  21.5 0.0 copy-done
  21.5 0.0 copy-done.3
  21.5 0.0 copy-done.4
  21.5 0.0 copy-done.1
  21.5 0.0 copy-done.2
  21.5 15.1 %fold.1 = (bf16[2,256,256]{2,1,0:T(8,128)(2,1)S(1)}, f32[5,128]{1,0:T(8,128)S(1)}) custom-call(bf16[2,2,2,256,256]{4,3,2,1,0:T(8,128)(2,1)S(1)} %get-tuple-element.8.data_ref, f32[2,2,256,256]{3,2,1,0:T(8,128)S(1)} %get-tuple-element.9.response_ref, s32[1,64]{1,0:T(1,128)S(1)} %copy-done.2, s32[512,128]{1,0:T(8,128)S(1)} %bitcast.13, ...), custom_call_target="tpu_custom_call" | custom-call | flops 6000000000 | bytes 6291456 | tf_op jit(solution)/shard_map/fold/pallas_call | solution.py:702
  36.6 0.8 %reshape.33 = bf16[2,1,65536]{2,0,1:T(2,128)(2,1)} reshape(bf16[2,256,256]{2,1,0:T(8,128)(2,1)S(1)} %get-tuple-element.10) | data formatting | bytes 524288 | tf_op jit(solution)/shard_map/reshape | solution.py:740
  37.4 0.5 %slice.9 = f32[1,64]{1,0:T(1,128)} slice(f32[5,128]{1,0:T(8,128)S(1)} %get-tuple-element.11), slice={[4:5], [0:64]} | slice | bytes 512 | tf_op jit(solution)/shard_map/slice | solution.py:741
  37.9 0.6 %slice_bitcast_fusion = (f32[256]{0:T(256)}, f32[2,128]{1,0:T(2,128)}) fusion(f32[5,128]{1,0:T(8,128)S(1)} %get-tuple-element.11), kind=kLoop, calls=%fused_computation | loop fusion | bytes 4096 | tf_op jit(solution)/shard_map/reshape | solution.py:743
Async XLA Ops:
  0.6 20.9 %copy-start = (f32[2,256,128]{2,1,0:T(8,128)S(1)}, f32[2,256,128]{2,1,0:T(8,128)}, u32[]{:S(2)}) copy-start(f32[2,256,128]{2,1,0:T(8,128)} %constant.6.clone.turns_hbm.turns_ref) | copy-start | bytes 786436
  0.6 20.9 %copy-start.3 = (f32[2,2,256,256]{3,2,1,0:T(8,128)S(1)}, f32[2,2,256,256]{3,2,1,0:T(8,128)}, u32[]{:S(2)}) copy-start(f32[2,2,256,256]{3,2,1,0:T(8,128)} %constant.8.clone.twist_ref) | copy-start | bytes 3145732
  0.7 20.8 %copy-start.4 = (bf16[2,768,256]{2,1,0:T(8,128)(2,1)S(1)}, bf16[2,768,256]{2,1,0:T(8,128)(2,1)}, u32[]{:S(2)}) copy-start(bf16[2,768,256]{2,1,0:T(8,128)(2,1)} %constant.7.clone.dft_ref) | copy-start | bytes 2359300
  0.7 20.8 %copy-start.1 = (s32[65536]{0:T(1024)S(1)}, s32[65536]{0:T(1024)}, u32[]{:S(2)}) copy-start(s32[65536]{0:T(1024)} %param.15) | copy-start | bytes 786436
  0.7 20.8 %copy-start.2 = (s32[1,64]{1,0:T(1,128)S(1)}, s32[1,64]{1,0:T(1,128)}, u32[]{:S(2)}) copy-start(s32[1,64]{1,0:T(1,128)} %flags_ref.1) | copy-start | bytes 772

commit v6 on v5

--- a/solution.py
+++ b/solution.py
@@ -30,9 +30,9 @@
 STEP_LINES = 8
 LANES = 128
 DEPTH = 256
-PARTS = 8
-PAIR_LAG = 2
-CHIP_LAG = 5
+PARTS = 4
+PAIR_LAG = 1
+CHIP_LAG = 2
 PART_ROWS = HALF_ROWS // PARTS
 MESH = pl.DeviceIdType.MESH
 
@@ -178,7 +178,8 @@
     size = vbuf.shape[3]
 
     levels = pairs.bit_length() - 1
-    roles = sorted(range(pairs), key=lambda role: (role & 1 == 0, -role))
+    roles = range(pairs)
+    halves = (range(1, pairs, 2), range(0, pairs, 2))
 
     def bit(level, side):
         return jnp.where(side == 0, 1 << level, 1 << (level + 1) % levels)
@@ -202,36 +203,40 @@
             volt_ref.at[:, pl.ds(start, size)], vbuf.at[part, slot], load_sem.at[part, slot]
         )
 
-    def begin(step, carry):
+    def begin(step, half):
         @pl.when(step < PARTS)
         def _():
-            for role in roles:
+            for role in halves[half]:
                 load(step, role, True).start()
 
         @pl.when(step >= PAIR_LAG)
         def _():
-            for role in roles:
+            for role in halves[half]:
                 load(step - PAIR_LAG, role, False).start()
 
-        return carry
+        return 0
 
     gains_copy = pltpu.make_async_copy(gains_hbm, gains_ref, side_sems.at[2])
     gains_copy.start()
-    lax.fori_loop(0, PARTS + PAIR_LAG, begin, 0)
+    for half in range(2):
+        lax.fori_loop(0, PARTS + PAIR_LAG, lambda step, carry, half=half: begin(step, half), 0)
     side = [
         pltpu.make_async_copy(chirp_hbm, chirp_ref, side_sems.at[0]),
         pltpu.make_async_copy(turns_hbm, turns_ref, side_sems.at[1]),
     ]
     for copy in side:
         copy.start()
-    offset = offset_ref[0]
     gains_copy.wait()
     weight_table(gains_ref, table_ref, antennas, me)
 
-    def pair_copy(part):
+    def place_of(role):
+        return role // 2 + (0 if role % 2 else pairs // 2)
+
+    def pair_copy(part, half):
+        slots = slice(half * (pairs // 2), (half + 1) * (pairs // 2))
         return pltpu.make_async_remote_copy(
-            src_ref=pair_send.at[part], dst_ref=pair_recv.at[part],
-            send_sem=pair_sems.at[0, part], recv_sem=pair_sems.at[1, part],
+            src_ref=pair_send.at[part, slots], dst_ref=pair_recv.at[part, slots],
+            send_sem=pair_sems.at[0, part, half], recv_sem=pair_sems.at[1, part, half],
             device_id={"tm": pair * 2 + (1 - core)}, device_id_type=MESH,
         )
 
@@ -325,74 +330,83 @@
             for out, value in enumerate(values):
                 data_ref[kind, out, 0, rows], data_ref[kind, out, 1, rows] = split(value)
 
-    def give(part):
-        for role in roles:
+    def give(part, half):
+        for role in halves[half]:
             load(part, role, True).wait()
-        for role in roles:
+        for role in halves[half]:
 
             def put(out, at, rows, value, role=role):
-                pair_send[part, role, out, at : at + rows] = value
+                pair_send[part, place_of(role), out, at : at + rows] = value
 
             part_beam(table_ref, vbuf.at[part, 2 * role], antennas, put)
-
-        @pl.when(part == 0)
-        def _():
-            pl.semaphore_wait(barrier, count - 1)
-
-        pair_copy(part).start()
-
-    def take(part):
-        for role in roles:
+        if half == 0:
+
+            @pl.when(part == 0)
+            def _():
+                pl.semaphore_wait(barrier, count - 1)
+
+        pair_copy(part, half).start()
+
+    def take(part, half):
+        for role in halves[half]:
             load(part, role, False).wait()
-        pair_copy(part).wait_recv()
-        for role in roles:
+        pair_copy(part, half).wait_recv()
+        for role in halves[half]:
 
             def put(out, at, rows, value, role=role):
-                value = value + pair_recv[part, role, out, at : at + rows]
+                value = value + pair_recv[part, place_of(role), out, at : at + rows]
                 if role % 2:
                     chip_send[part, slot_of(role), out, at : at + rows] = value.astype(jnp.bfloat16)
                 else:
                     own_ref[part, role // 2, out, at : at + rows] = value
 
             part_beam(table_ref, vbuf.at[part, 2 * role + 1], antennas, put)
-        chip_copy(part, 0).start()
-
-    def run(step, carry):
+        if half == 0:
+            chip_copy(part, 0).start()
+
+    def run(step, half):
         @pl.when(step < PARTS)
         def _():
-            give(step)
-
-        @pl.when(step >= PAIR_LAG)
+            give(step, half)
+
+        @pl.when((step >= PAIR_LAG) & (step < PARTS + PAIR_LAG))
         def _():
-            take(step - PAIR_LAG)
-
+            take(step - PAIR_LAG, half)
+
+    def spread(step, carry):
+        run(step, 0)
         return carry
 
-    lax.fori_loop(0, PARTS + PAIR_LAG, run, 0)
+    def gather(step, carry):
+        run(step, 1)
+
+        @pl.when(step >= CHIP_LAG)
+        def _():
+            for level in range(levels - 1):
+                pass_on(step - CHIP_LAG, level)
+
+        return carry
+
+    lax.fori_loop(0, PARTS + PAIR_LAG, spread, 0)
+    lax.fori_loop(0, PARTS + CHIP_LAG, gather, 0)
     for copy in side:
         copy.wait()
+    offset = offset_ref[0]
 
     def settle(step, carry):
-        @pl.when(step < PARTS)
+        finish(step)
+
+        @pl.when((step == 0) & (me > 0))
         def _():
-            for level in range(levels - 1):
-                pass_on(step, level)
+            head_copy().start()
 
         @pl.when(step < ROWS // LANES)
         def _():
             chirp_block(step)
 
-        @pl.when(step >= CHIP_LAG)
-        def _():
-            finish(step - CHIP_LAG)
-
-            @pl.when((step == CHIP_LAG) & (me > 0))
-            def _():
-                head_copy().start()
-
         return carry
 
-    lax.fori_loop(0, PARTS + CHIP_LAG, settle, 0)
+    lax.fori_loop(0, PARTS, settle, 0)
 
     @pl.when(me == 0)
     def _():
@@ -437,7 +451,8 @@
             halo_copy(part).wait_send()
 
     def drain(part, carry):
-        pair_copy(part).wait_send()
+        for half in range(2):
+            pair_copy(part, half).wait_send()
         for level in range(levels):
             chip_copy(part, level).wait_send()
         return carry
@@ -478,7 +493,7 @@
             pltpu.VMEM((2, HALF_ROWS, LANES), jnp.float32),
             pltpu.VMEM((LANES, LANES), jnp.float32),
             pltpu.SemaphoreType.DMA((PARTS, shards)),
-            pltpu.SemaphoreType.DMA((2, PARTS)),
+            pltpu.SemaphoreType.DMA((2, PARTS, 2)),
             pltpu.SemaphoreType.DMA((2, PARTS, pairs.bit_length() - 1)),
             pltpu.SemaphoreType.DMA((2, PARTS)),
             pltpu.SemaphoreType.DMA((2,)),
@@ -494,25 +509,10 @@
     )(keep(volts), keep(gains), offset, keep(chirp), keep(jnp.asarray(half_turns())))
 
 
-def fold_kernel(
-    chans, shards, data_ref, response_ref, flags_ref, bins_ref, dft_ref, twist_ref, turns_ref,
-    dedispersed_ref, small_ref, weighted_ref, high_ref, low_ref, send_ref, recv_ref,
-    sems,
+def spectrum_kernel(
+    data_ref, response_ref, flags_ref, dft_ref, twist_ref, turns_ref, dedispersed_ref, weight_ref,
+    weighted_ref, blend_ref,
 ):
-    everyone = chans * shards
-    here = lax.axis_index("chan") * shards + lax.axis_index("tm")
-    barrier = pltpu.get_barrier_semaphore()
-
-    def target(index):
-        return {"chan": index // shards, "tm": lax.rem(index, shards)}
-
-    def greet(step, carry):
-        pl.semaphore_signal(
-            barrier, inc=1, device_id=target(lax.rem(here + step, everyone)), device_id_type=MESH
-        )
-        return carry
-
-    lax.fori_loop(1, everyone, greet, 0)
     def table(start, count=1):
         rows = slice(start * COLS, (start + count) * COLS)
         return (dft_ref[0, rows], dft_ref[1, rows])
@@ -580,8 +580,14 @@
         (real, imag), (odd_real, odd_imag) = [[value[rows] for value in pair] for pair in pairs]
         real = real - (odd_real * cosine + odd_imag * sine)
         imag = imag - (odd_imag * cosine - odd_real * sine)
-        dedispersed_ref[0, rows] = real.astype(jnp.bfloat16)
-        dedispersed_ref[1, rows] = imag.astype(jnp.bfloat16)
+        for out, value in enumerate((real, imag)):
+            for at in range(per_line):
+                places = pl.ds(2 * at + out, BLOCK_ROWS, stride=2 * per_line)
+                blend_ref[places, :] = value[:, at * LANES : (at + 1) * LANES]
+        lines = 2 * per_line * BLOCK_ROWS
+        dedispersed_ref[start * 2 * per_line : start * 2 * per_line + lines] = blend_ref[
+            ...
+        ].astype(jnp.bfloat16)
         power = real * real + imag * imag
         first_sum, second_sum = (window_sum(power), window_sum(power * power))
         kurtosis = (
@@ -604,9 +610,32 @@
             places = pl.ds(start * per_line + at, BLOCK_ROWS, stride=per_line)
             weighted_ref[places, :] = value.astype(jnp.float32)
 
+    weight_ref[...] = weight_row[:, :WINDOWS]
+
+
+def fold_kernel(
+    chans, shards, weighted_ref, bins_ref, small_ref, high_ref, low_ref, send_ref, recv_ref, sems
+):
+    everyone = chans * shards
+    mine = lax.axis_index("chan")
+    here = mine * shards + lax.axis_index("tm")
+    barrier = pltpu.get_barrier_semaphore()
+
+    def target(index):
+        return {"chan": index // shards, "tm": lax.rem(index, shards)}
+
+    def greet(step, carry):
+        pl.semaphore_signal(
+            barrier, inc=1, device_id=target(lax.rem(here + step, everyone)), device_id_type=MESH
+        )
+        return carry
+
+    lax.fori_loop(1, everyone, greet, 0)
+    per_line = COLS // LANES
     bins = bins_ref[...]
-    high_ref[...] = (bins // LOW_BINS).astype(jnp.float32)
-    low_ref[...] = (bins % LOW_BINS).astype(jnp.float32)
+    shift = LOW_BINS.bit_length() - 1
+    high_ref[...] = lax.shift_right_logical(bins, jnp.full_like(bins, shift)).astype(jnp.float32)
+    low_ref[...] = (bins & (LOW_BINS - 1)).astype(jnp.float32)
     high_index = lax.broadcasted_iota(jnp.int32, (HIGH_BINS, LANES), 0)
     high_index = high_index.astype(jnp.float32).astype(jnp.bfloat16)
     low_index = lax.broadcasted_iota(jnp.int32, (LOW_BINS, LANES), 0)
@@ -681,7 +710,6 @@
     lax.fori_loop(1, everyone, arrive, 0)
     scale = BINS / (HALF_ROWS * COLS * shards)
     band = None
-    mine = lax.axis_index("chan")
     for chan in range(chans):
         line = recv_ref[chan * shards]
         for at in range(1, shards):
@@ -691,38 +719,52 @@
         band, profile = (line, own) if band is None else (band + line, profile + own)
     small_ref[0:lines] = profile
     small_ref[lines : 2 * lines] = band
-    small_ref[2 * lines : 2 * lines + 1] = weight_row
     lax.fori_loop(1, everyone, leave, 0)
 
 
-def fold(data, reply, flags, bins, chans, shards):
+def spectrum(data, reply, flags):
     vmem = pl.BlockSpec(memory_space=pltpu.VMEM)
     tables = (dft_table(), twiddle(), half_turns())
+    lines = HALF_ROWS * COLS // LANES
+    return pl.pallas_call(
+        spectrum_kernel,
+        out_shape=(
+            jax.ShapeDtypeStruct((2 * lines, LANES), jnp.bfloat16),
+            jax.ShapeDtypeStruct((1, WINDOWS), jnp.float32),
+            jax.ShapeDtypeStruct((lines, LANES), jnp.float32),
+        ),
+        in_specs=[vmem] * 6,
+        out_specs=(vmem,) * 3,
+        scratch_shapes=[pltpu.VMEM((2 * BLOCK_ROWS * COLS // LANES, LANES), jnp.float32)],
+        compiler_params=pltpu.CompilerParams(vmem_limit_bytes=40 << 20),
+        cost_estimate=pl.CostEstimate(
+            flops=5 * 10**9, bytes_accessed=6 << 20, transcendentals=0
+        ),
+        name="spectrum",
+    )(data, reply, flags, *[jnp.asarray(table) for table in tables])
+
+
+def fold(weighted, bins, chans, shards):
+    vmem = pl.BlockSpec(memory_space=pltpu.VMEM)
     lines = BINS // LANES // shards
     return pl.pallas_call(
         functools.partial(fold_kernel, chans, shards),
-        out_shape=(
-            jax.ShapeDtypeStruct((2, HALF_ROWS, COLS), jnp.bfloat16),
-            jax.ShapeDtypeStruct((2 * lines + 1, LANES), jnp.float32),
-        ),
-        in_specs=[vmem] * 7,
-        out_specs=(vmem,) * 2,
+        out_shape=jax.ShapeDtypeStruct((2 * lines, LANES), jnp.float32),
+        in_specs=[vmem, vmem],
+        out_specs=vmem,
         scratch_shapes=[
-            pltpu.VMEM((HALF_ROWS * COLS // LANES, LANES), jnp.float32),
-            pltpu.VMEM((HALF_ROWS * COLS // LANES, LANES), jnp.float32),
-            pltpu.VMEM((HALF_ROWS * COLS // LANES, LANES), jnp.float32),
+            pltpu.VMEM(bins.shape, jnp.float32),
+            pltpu.VMEM(bins.shape, jnp.float32),
             pltpu.VMEM((shards, lines, LANES), jnp.float32),
             pltpu.VMEM((chans * shards, lines, LANES), jnp.float32),
             pltpu.SemaphoreType.DMA((2, chans * shards)),
         ],
         compiler_params=pltpu.CompilerParams(
-            vmem_limit_bytes=40 << 20, collective_id=1, has_side_effects=True
+            vmem_limit_bytes=16 << 20, collective_id=1, has_side_effects=True
         ),
-        cost_estimate=pl.CostEstimate(
-            flops=6 * 10**9, bytes_accessed=6 << 20, transcendentals=0
-        ),
+        cost_estimate=pl.CostEstimate(flops=10**9, bytes_accessed=1 << 20, transcendentals=0),
         name="fold",
-    )(data, reply, flags, bins, *[jnp.asarray(table) for table in tables])
+    )(weighted, bins)
 
 
 def on_device(voltages, antenna_gains, chirp_phase, offsets, flags, sample_phase_bins):
@@ -734,13 +776,15 @@
     gains = jnp.transpose(antenna_gains, (0, 2, 1))
     data, reply = beam(volts, gains, offsets, chirp_phase.reshape(-1, LANES), shards)
     bins = sample_phase_bins.reshape(-1, LANES)
-    dedispersed, small = fold(data, reply, flags, bins, chans, shards)
+    dedispersed, weight, weighted = spectrum(data, reply, flags)
+    small = fold(weighted, bins, chans, shards)
     lines = BINS // LANES // shards
+    dedispersed = jnp.transpose(dedispersed.reshape(-1, 2, LANES), (1, 0, 2))
     return (
         dedispersed.reshape(2, 1, HALF_ROWS * COLS),
-        small[2 * lines : 2 * lines + 1, :WINDOWS],
+        weight,
         small[:lines].reshape(1, BINS // shards),
-        small[lines : 2 * lines].reshape(BINS // shards),
+        small[lines:].reshape(BINS // shards),
     )
 
 

time: 38.7 us -> 37.3 us (0.964)
  local copies, waits for them, and re-layouts: 1.88 us -> 0.6 us
    pallas_call x1, Pallas kernels: 20 us -> 18.8 us  [beam(): pl.pallas_call(functools.partial(beam_kernel, antennas, pairs), out_shape...]
    pallas_call x1 -> x2, Pallas kernels: 15.1 us -> 16.2 us  [the longest x1 11.5 us: fold(): pl.pallas_call(functools.partial(fold_kernel, chans, shards), out_shape=j...]
    reshape x2 -> x1, local copies, waits for them, and re-layouts: 1.34 us -> 0.57 us  [on_device(): small[lines:].reshape(BINS // shards)]
    slice x1 -> x0, local copies, waits for them, and re-layouts: 0.51 us -> none  [on_device(): small[2 * lines:2 * lines + 1, :WINDOWS]]
where the time goes in v6:
time: 37.3 us; the launch traced here: 37.1 us
  Pallas kernels  35 us (94%)
  between operations  1.51 us (4%)
  local copies, waits for them, and re-layouts  0.6 us (2%)
    pallas_call x1, Pallas kernels, beam(): pl.pallas_call(functools.partial(beam_kernel, antennas, pairs), out_shape...  18.8 us
    pallas_call x1, Pallas kernels, fold(): pl.pallas_call(functools.partial(fold_kernel, chans, shards), out_shape=j...  11.5 us
    pallas_call x1, Pallas kernels, spectrum(): pl.pallas_call(spectrum_kernel, out_shape=(jax.ShapeDtypeStruct((2 * line...  4.66 us

profile of v6, /device:TPU:0, one launch (start us, length us, event | category | flops | bytes accessed | tf_op | source)
XLA Modules:
  0.0 37.1 jit_solution(16739190191671878559)
XLA Ops:
  0.6 0.0 copy-start
  0.6 0.0 copy-start.3
  0.7 0.0 copy-start.4
  0.7 0.0 copy-start.2
  1.5 0.0 copy-start.1
  1.5 18.8 %beam.1 = (bf16[2,2,2,256,256]{4,3,2,1,0:T(8,128)(2,1)S(1)}, f32[2,2,256,256]{3,2,1,0:T(8,128)S(1)}) custom-call(bf16[2,32768,128]{2,1,0:T(8,128)(2,1)} %bitcast.19, f32[2,1,64]{2,1,0:T(1,128)} %bitcast.22, s32[1]{0:T(128)S(6)} %copy.16.offset_ref, f32[1024,128]{1,0:T(8,128)} %bitcast.20, f32[2,256,128]{2,1,0:T(8,128)} %constant.6.clone.turns_hbm.turns_ref), custom_call_target="tpu_custom_call" | custom-call | flops 3000000000 | bytes 18874368 | tf_op jit(solution)/shard_map/beam/pallas_call | solution.py:472
  20.3 0.0 copy-done
  20.3 0.0 copy-done.3
  20.3 0.0 copy-done.4
  20.4 0.0 copy-done.2
  20.4 4.7 %spectrum.1 = (bf16[1024,128]{1,0:T(8,128)(2,1)}, f32[1,64]{1,0:T(1,128)}, f32[512,128]{1,0:T(8,128)S(1)}) custom-call(bf16[2,2,2,256,256]{4,3,2,1,0:T(8,128)(2,1)S(1)} %get-tuple-element.9.data_ref, f32[2,2,256,256]{3,2,1,0:T(8,128)S(1)} %get-tuple-element.10.response_ref, s32[1,64]{1,0:T(1,128)S(1)} %copy-done.2, bf16[2,768,256]{2,1,0:T(8,128)(2,1)S(1)} %copy-done.4, ...), custom_call_target="tpu_custom_call" | custom-call | flops 5000000000 | bytes 6291456 | tf_op jit(solution)/shard_map/spectrum/pallas_call | solution.py:729
  25.0 0.0 copy-done.1
  25.0 11.5 %fold.1 = f32[4,128]{1,0:T(4,128)S(1)} custom-call(f32[512,128]{1,0:T(8,128)S(1)} %get-tuple-element.13.weighted_ref, s32[512,128]{1,0:T(8,128)S(1)} %bitcast.18), custom_call_target="tpu_custom_call" | custom-call | flops 1000000000 | bytes 1048576 | tf_op jit(solution)/shard_map/fold/pallas_call | solution.py:750
  36.6 0.6 %slice_bitcast_fusion = (f32[256]{0:T(256)}, f32[2,128]{1,0:T(2,128)}) fusion(f32[4,128]{1,0:T(4,128)S(1)} %fold.1), kind=kLoop, calls=%fused_computation | loop fusion | bytes 4096 | tf_op jit(solution)/shard_map/reshape | solution.py:787
Async XLA Ops:
  0.6 19.7 %copy-start = (f32[2,256,128]{2,1,0:T(8,128)S(1)}, f32[2,256,128]{2,1,0:T(8,128)}, u32[]{:S(2)}) copy-start(f32[2,256,128]{2,1,0:T(8,128)} %constant.6.clone.turns_hbm.turns_ref) | copy-start | bytes 786436
  0.6 19.7 %copy-start.3 = (f32[2,2,256,256]{3,2,1,0:T(8,128)S(1)}, f32[2,2,256,256]{3,2,1,0:T(8,128)}, u32[]{:S(2)}) copy-start(f32[2,2,256,256]{3,2,1,0:T(8,128)} %constant.8.clone.twist_ref) | copy-start | bytes 3145732
  0.7 19.7 %copy-start.4 = (bf16[2,768,256]{2,1,0:T(8,128)(2,1)S(1)}, bf16[2,768,256]{2,1,0:T(8,128)(2,1)}, u32[]{:S(2)}) copy-start(bf16[2,768,256]{2,1,0:T(8,128)(2,1)} %constant.7.clone.dft_ref) | copy-start | bytes 2359300
  0.7 19.7 %copy-start.2 = (s32[1,64]{1,0:T(1,128)S(1)}, s32[1,64]{1,0:T(1,128)}, u32[]{:S(2)}) copy-start(s32[1,64]{1,0:T(1,128)} %flags_ref.1) | copy-start | bytes 772
  1.5 23.6 %copy-start.1 = (s32[65536]{0:T(1024)S(1)}, s32[65536]{0:T(1024)}, u32[]{:S(2)}) copy-start(s32[65536]{0:T(1024)} %param.15) | copy-start | bytes 786436
